TPU v7x, 32 devices: a whole 2x2x4 slice. The times are simulated.
32 devices in a mesh: col: 16 (over z, y, x), sec: 2 (over core).
Axes of the slice: x: 2, y: 2, z: 4, core: 2. Of those that a mesh axis runs over, the one named last changes fastest.
Arguments:
- mps: bfloat16 [16, 96, 6, 6, 96], P('col', 'sec'), may hold values from -6 to 6
- ket: bfloat16 [16, 6, 6, 6, 6, 2], P('col'), may hold values from -6 to 6
- left_proj: bfloat16 [16, 96, 96, 6, 6], P('col', 'sec'), may hold values from -0.109375 to 0.109375
- right_proj: bfloat16 [16, 96, 6, 6, 96], P('col', None, None, None, 'sec'), may hold values from -0.109375 to 0.109375
- bond_charge: int32 [16, 96], P('col'), may hold values from 0 to 5
- new_charge: int32 [16, 96], P('col'), may hold values from 0 to 5
- link_charge: int32 [16, 6], P('col'), may hold values from 0 to 2
- vert_charge: int32 [16, 2, 6], P('col'), may hold values from 0 to 2
Outputs:
- new_mps: bfloat16 [16, 96, 6, 6, 96], P('col', 'sec')
- log_norm: float32 [], replicated
All inputs are finite; a program needn't handle non-finite values.
Results may differ from a plain program's by a relative error of at most 0.0064.
Values may be sent and summed in bfloat16 or wider, within the bound.
No kernel may reach another device: no remote copies, remote signals or barrier semaphores. Data moves between devices by JAX's collectives and lax.ppermute only.
A program may use at most 192 MiB of HBM per device.

v0:
```python
import jax
import jax.numpy as jnp
from jax import lax
from jax.sharding import PartitionSpec as P


def from_behind(x, axis, by):
    count = lax.axis_size(axis)
    return lax.ppermute(x, axis, [(i, (i + by) % count) for i in range(count)])


def absorb(
    mps_site,
    ket_site,
    left_site,
    right_site,
    charge_here,
    charge_next,
    fresh_here,
    fresh_next,
    link_here,
    link_next,
    vertical,
):
    upper = vertical[0]
    lower = vertical[1]
    physical = jnp.arange(ket_site.shape[4], dtype=jnp.int32)
    keep_mps = (
        charge_here[:, None, None, None] + upper[None, :, None, None] - upper[None, None, :, None]
        == charge_next[None, None, None, :]
    )
    masked_mps = jnp.where(keep_mps, mps_site, jnp.zeros_like(mps_site))
    keep_ket = (
        upper[:, None, None, None, None] + link_here[None, :, None, None, None]
        == lower[None, None, :, None, None]
        + link_next[None, None, None, :, None]
        + physical[None, None, None, None, :]
    )
    masked_ket = jnp.where(keep_ket, ket_site, jnp.zeros_like(ket_site))
    keep_left = (
        fresh_here[:, None, None, None]
        == charge_here[None, :, None, None]
        + link_here[None, None, :, None]
        - link_here[None, None, None, :]
    )
    masked_left = jnp.where(keep_left, left_site, jnp.zeros_like(left_site))
    keep_right = (
        charge_next[:, None, None, None]
        + link_next[None, :, None, None]
        - link_next[None, None, :, None]
        == fresh_next[None, None, None, :]
    )
    masked_right = jnp.where(keep_right, right_site, jnp.zeros_like(right_site))
    first = jnp.einsum(
        "xalm,auvb->xlmuvb", masked_left, masked_mps, preferred_element_type=jnp.float32
    ).astype(jnp.bfloat16)
    second = jnp.einsum(
        "xlmuvb,uldrp->xmvbdrp", first, masked_ket, preferred_element_type=jnp.float32
    ).astype(jnp.bfloat16)
    third = jnp.einsum(
        "xmvbdrp,vmesp->xbdres", second, masked_ket, preferred_element_type=jnp.float32
    ).astype(jnp.bfloat16)
    return jnp.einsum("xbdres,brsy->xdey", third, masked_right, preferred_element_type=jnp.float32)


def local(mps, ket, left_proj, right_proj, bond_charge, new_charge, link_charge, vert_charge):
    sites_here = mps.shape[0]
    half = left_proj.shape[1]
    full_mps = lax.all_gather(mps, "sec", axis=1, tiled=True)
    chi_full = full_mps.shape[1]
    legs = full_mps.shape[2]
    received = from_behind((bond_charge, new_charge, link_charge), "col", -1)
    bond_next = jnp.concatenate([bond_charge[1:], received[0]], axis=0)
    fresh_next = jnp.concatenate([new_charge[1:], received[1]], axis=0)
    link_next = jnp.concatenate([link_charge[1:], received[2]], axis=0)
    arrived = from_behind(right_proj, "col", -1)
    partial_next = jnp.concatenate([right_proj[1:], arrived], axis=0)
    right_next = lax.all_gather(partial_next, "sec", axis=4, tiled=True)
    offset = lax.axis_index("sec") * half
    fresh_half = lax.dynamic_slice_in_dim(new_charge[0], offset, half, 0)
    images = [
        absorb(
            full_mps[0],
            ket[0],
            left_proj[0],
            right_next[0],
            bond_charge[0],
            bond_next[0],
            fresh_half,
            fresh_next[0],
            link_charge[0],
            link_next[0],
            vert_charge[0],
        )
    ]
    image = jnp.stack(images, axis=0)
    partial_value = jnp.sum(image * image, axis=(1, 2, 3, 4))
    count = chi_full * legs * legs * chi_full
    columns = lax.axis_size("col")
    squares = lax.psum(partial_value, "sec")
    meansq = squares / count
    logs = 0.5 * jnp.log(meansq + 1e-06)
    total = lax.psum(jnp.sum(logs), "col")
    log_norm = total / (sites_here * columns)
    scale = lax.rsqrt(meansq + 1e-06)
    new_mps = (image * scale[:, None, None, None, None]).astype(jnp.bfloat16)
    return (new_mps, log_norm)


def solution(mesh):
    placed = (
        P("col", "sec", None, None, None),
        P("col", None, None, None, None, None),
        P("col", "sec", None, None, None),
        P("col", None, None, None, "sec"),
        P("col", None),
        P("col", None),
        P("col", None),
        P("col", None, None),
    )
    return jax.shard_map(
        local,
        mesh=mesh,
        in_specs=placed,
        out_specs=(P("col", "sec", None, None, None), P()),
        check_vma=False,
    )
```

profile of v0, /device:TPU:0, one launch (start us, length us, event | category | flops | bytes accessed | tf_op | source)
XLA Modules:
  0.0 157.0 jit_solution(7892534754930286098)
XLA Ops:
  0.6 7.0 %collective-permute-start = (s32[1,96]{1,0:T(1,128)}, s32[1,96]{1,0:T(1,128)S(1)}, u32[]{:S(2)}, u32[]{:S(2)}) collective-permute-start(s32[1,96]{1,0:T(1,128)} %param.12), channel_id=1, source_target_pairs={{0,30},{2,0},{4,2},{6,4},{8,6},{10,8},{12,10},{14,12},{16,14},{18,... | collective-permute-start | bytes 1160 | tf_op jit(solution)/shard_map/ppermute | solution.py:9
  7.6 0.5 collective-permute-start.1
  8.2 1.4 collective-permute-start.3
  9.6 0.5 collective-permute-start.2
  10.1 0.8 slice_bitcast_fusion
  10.9 0.7 broadcast_add_fusion.2
  11.6 0.7 broadcast_add_fusion.4
  12.4 0.1 broadcast_subtract_fusion.1
  12.4 0.7 broadcast_subtract_fusion.2
  13.2 0.7 dynamic-slice_bitcast_fusion
  13.9 2.6 %all_gather.6 = bf16[1,96,6,6,96]{4,1,3,2,0:T(8,128)(2,1)S(1)} all-gather(bf16[1,48,6,6,96]{4,1,3,2,0:T(8,128)(2,1)} %param.8), channel_id=1, replica_groups=mesh['col'=16,'sec'=2] {'sec'}, dimensions={1}, use_global_device_ids=true | all-gather | bytes 995328 | tf_op jit(solution)/shard_map/all_gather | solution.py:69
  16.5 0.1 broadcast_add_fusion.1
  16.6 1.1 fusion.30
  17.8 0.0 collective-permute-done
  17.8 5.7 %convert_bitcast_fusion = bf16[48,6,6,6,6,96,1,1]{5,0,4,3,2,1,7,6:T(8,128)(2,1)S(1)} fusion(bf16[1,96,6,6,96]{4,1,3,2,0:T(8,128)(2,1)S(1)} %all_gather.6, s32[96]{0:T(128)S(1)} %bitcast.70, s32[96,6,6]{0,2,1:T(8,128)S(1)} %broadcast_subtract_fusion.1, bf16[1,48,96,6,6]{2,1,4,3,0:T(8,128)(2,1)} %param.10, s32[96,6,6]{0,2,1:T(8,128)S(1)} %broadcast_subtract_fusion.2, ...), kind=kOutput, calls=%fused_computation.8 | convolution fusion | flops 1153585152 | bytes 12967488 | tf_op jit(solution)/shard_map/xalm,auvb->xlmuvb/dot_general | solution.py:54
  23.4 28.1 %fusion = bf16[48,6,6,96,6,6,2,1]{3,5,6,4,2,1,0,7:T(8,128)(2,1)} fusion(bf16[48,6,6,6,6,96,1,1]{5,0,4,3,2,1,7,6:T(8,128)(2,1)S(1)} %convert_bitcast_fusion, bf16[6,6,6,6,2,1,1,1]{3,4,2,1,0,7,6,5:T(2,128)(2,1)S(1)} %fusion.30), kind=kOutput, calls=%fused_computation.1 | convolution fusion | flops 871907328 | bytes 35836992 | tf_op jit(solution)/shard_map/xlmuvb,uldrp->xmvbdrp/dot_general | solution.py:57
  51.5 38.6 %bitcast_convert_fusion.1 = bf16[48,96,6,6,6,6]{1,5,4,3,2,0:T(8,128)(2,1)} fusion(bf16[48,6,6,96,6,6,2,1]{3,5,6,4,2,1,0,7:T(8,128)(2,1)} %fusion, bf16[6,6,6,6,2,1,1,1]{3,4,2,1,0,7,6,5:T(2,128)(2,1)S(1)} %fusion.30), kind=kOutput, calls=%fused_computation.2 | convolution fusion | flops 865935360 | bytes 35836992 | tf_op jit(solution)/shard_map/xmvbdrp,vmesp->xbdres/dot_general | solution.py:60
  90.1 0.1 broadcast_add_fusion
  90.2 0.1 broadcast_subtract_fusion
  90.2 2.8 %all_gather.7 = bf16[1,96,6,6,96]{1,4,3,2,0:T(8,128)(2,1)S(1)} all-gather(bf16[1,96,6,6,48]{1,4,3,2,0:T(8,128)(2,1)} %collective-permute-done.3), channel_id=1, replica_groups=mesh['col'=16,'sec'=2] {'sec'}, dimensions={4}, use_global_device_ids=true | all-gather | bytes 995328 | tf_op jit(solution)/shard_map/all_gather | solution.py:78
  93.1 17.4 %multiply_reduce_fusion = (f32[]{:T(128)}, f32[48,6,6,96]{3,0,2,1:T(8,128)S(1)}) fusion(bf16[1,96,6,6,96]{1,4,3,2,0:T(8,128)(2,1)S(1)} %all_gather.7, s32[96,6,6]{0,2,1:T(8,128)S(1)} %broadcast_subtract_fusion, s32[96]{0:T(128)S(1)} %bitcast.73, bf16[48,96,6,6,6,6]{1,5,4,3,2,0:T(8,128)(2,1)} %bitcast_convert_fusion.1), kind=kOutput, calls=%fused_computation.16 | convolution fusion | flops 1147613184 | bytes 13285252 | tf_op jit(solution)/shard_map/xbdres,brsy->xdey/dot_general | solution.py:63
  110.4 3.1 %psum.14 = f32[1]{0:T(128)} all-reduce(f32[1]{0:T(128)} %bitcast.28), channel_id=1, replica_groups=mesh['col'=16,'sec'=2] {'sec'}, use_global_device_ids=true, to_apply=%region_1.2 | all-reduce | flops 1 | bytes 8 | tf_op jit(solution)/shard_map/psum | solution.py:100
  114.2 40.1 %psum.15 = f32[]{:T(128)} all-reduce(f32[]{:T(128)} %bitcast.31), channel_id=1, replica_groups=mesh['col'=16,'sec'=2] {'col'}, use_global_device_ids=true, to_apply=%region_2.3 | all-reduce | flops 1 | bytes 8 | tf_op jit(solution)/shard_map/psum | solution.py:103
  154.3 0.8 fusion.22
  (4 shorter events, 0.0 us)
Async XLA Ops:
  0.6 17.1 %collective-permute-start = (s32[1,96]{1,0:T(1,128)}, s32[1,96]{1,0:T(1,128)S(1)}, u32[]{:S(2)}, u32[]{:S(2)}) collective-permute-start(s32[1,96]{1,0:T(1,128)} %param.12), channel_id=1, source_target_pairs={{0,30},{2,0},{4,2},{6,4},{8,6},{10,8},{12,10},{14,12},{16,14},{18,... | collective-permute-start | bytes 1160 | tf_op jit(solution)/shard_map/ppermute | solution.py:9
  7.6 8.9 %collective-permute-start.1 = (s32[1,6]{1,0:T(1,128)}, s32[1,6]{1,0:T(1,128)S(1)}, u32[]{:S(2)}, u32[]{:S(2)}) collective-permute-start(s32[1,6]{1,0:T(1,128)} %param.14), channel_id=1, source_target_pairs={{0,30},{2,0},{4,2},{6,4},{8,6},{10,8},{12,10},{14,12},{16,14},{18,... | collective-permute-start | bytes 80 | tf_op jit(solution)/shard_map/ppermute | solution.py:9
  8.2 82.0 %collective-permute-start.3 = (bf16[1,96,6,6,48]{1,4,3,2,0:T(8,128)(2,1)}, bf16[1,96,6,6,48]{1,4,3,2,0:T(8,128)(2,1)}, u32[]{:S(2)}, u32[]{:S(2)}) collective-permute-start(bf16[1,96,6,6,48]{1,4,3,2,0:T(8,128)(2,1)} %param.11), channel_id=1, source_target_pairs={{0,30},{2,0},{4,2},{6,4},{8,6},{10,8},{12,10},{14,12},{16,14},{18,... | collective-permute-start | bytes 995336 | tf_op jit(solution)/shard_map/ppermute | solution.py:9
  9.6 83.4 %collective-permute-start.2 = (s32[1,96]{1,0:T(1,128)}, s32[1,96]{1,0:T(1,128)S(1)}, u32[]{:S(2)}, u32[]{:S(2)}) collective-permute-start(s32[1,96]{1,0:T(1,128)} %param.13), channel_id=1, source_target_pairs={{0,30},{2,0},{4,2},{6,4},{8,6},{10,8},{12,10},{14,12},{16,14},{18,... | collective-permute-start | bytes 1160 | tf_op jit(solution)/shard_map/ppermute | solution.py:9
where the time goes:
time: 157 us
  matrix products  89.7 us (57%)
  blocking collectives  48.6 us (31%)
  starting transfers between devices  9.52 us (6%)
  other arithmetic  4.45 us (3%)
  between operations  3.22 us (2%)
    psum x1, blocking collectives, local(): total = lax.psum(jnp.sum(logs), 'col')  40.1 us
    dot_general x1, matrix products, absorb(): jnp.einsum('xmvbdrp,vmesp->xbdres', second, masked_ket, preferred_element...  38.6 us
    dot_general x1, matrix products, absorb(): jnp.einsum('xlmuvb,uldrp->xmvbdrp', first, masked_ket, preferred_element_...  28.1 us
    dot_general x1, matrix products, absorb(): jnp.einsum('xbdres,brsy->xdey', third, masked_right, preferred_element_ty...  17.4 us
    ppermute x4, starting transfers between devices, from_behind(): return lax.ppermute(x, axis, [(i, (i + by) % count) for i in range(count)])  9.52 us
    dot_general x1, matrix products, absorb(): jnp.einsum('xalm,auvb->xlmuvb', masked_left, masked_mps, preferred_elemen...  5.67 us
  transfers between devices with their start and end apart: 4, of which 0 were waited for; matrix products, arithmetic and copies ran while one was open for 49% of the time, Pallas kernels for 0%

commit v1 on v0

--- a/solution.py
+++ b/solution.py
@@ -69,7 +69,10 @@
     full_mps = lax.all_gather(mps, "sec", axis=1, tiled=True)
     chi_full = full_mps.shape[1]
     legs = full_mps.shape[2]
-    received = from_behind((bond_charge, new_charge, link_charge), "col", -1)
+    chi = bond_charge.shape[1]
+    packed = jnp.concatenate([bond_charge, new_charge, link_charge], axis=1)
+    shifted = from_behind(packed, "col", -1)
+    received = (shifted[:, :chi], shifted[:, chi : 2 * chi], shifted[:, 2 * chi :])
     bond_next = jnp.concatenate([bond_charge[1:], received[0]], axis=0)
     fresh_next = jnp.concatenate([new_charge[1:], received[1]], axis=0)
     link_next = jnp.concatenate([link_charge[1:], received[2]], axis=0)
@@ -94,14 +97,16 @@
         )
     ]
     image = jnp.stack(images, axis=0)
-    partial_value = jnp.sum(image * image, axis=(1, 2, 3, 4))
+    partial_value = jnp.sum(image * image)
     count = chi_full * legs * legs * chi_full
     columns = lax.axis_size("col")
-    squares = lax.psum(partial_value, "sec")
-    meansq = squares / count
-    logs = 0.5 * jnp.log(meansq + 1e-06)
-    total = lax.psum(jnp.sum(logs), "col")
-    log_norm = total / (sites_here * columns)
+    sections = lax.axis_size("sec")
+    outgoing = jnp.broadcast_to(partial_value, (columns * sections, 1, 128))
+    incoming = lax.all_to_all(outgoing, ("col", "sec"), 0, 0, tiled=True)
+    squares = jnp.sum(incoming[:, 0, 0].reshape(columns, sections), axis=1)
+    meansq_all = squares / count
+    log_norm = jnp.sum(0.5 * jnp.log(meansq_all + 1e-06)) / (sites_here * columns)
+    meansq = lax.dynamic_slice_in_dim(meansq_all, lax.axis_index("col"), 1, 0)
     scale = lax.rsqrt(meansq + 1e-06)
     new_mps = (image * scale[:, None, None, None, None]).astype(jnp.bfloat16)
     return (new_mps, log_norm)

time: 157 us -> 127 us (0.81)
  blocking collectives: 48.6 us -> 7.02 us
  waiting for transfers between devices: 0.01 us -> 7.1 us
  local copies, waits for them, and re-layouts: 1.48 us -> 3.87 us
    psum x2 -> x0, blocking collectives: 43.2 us -> none  [the longest x1 40.1 us: local(): total = lax.psum(jnp.sum(logs), 'col')]
    all_to_all x0 -> x1, waiting for transfers between devices: none -> 7.1 us  [local(): incoming = lax.all_to_all(outgoing, ('col', 'sec'), 0, 0, tiled=True)]
    all_to_all x0 -> x1, starting transfers between devices: none -> 2.54 us  [local(): incoming = lax.all_to_all(outgoing, ('col', 'sec'), 0, 0, tiled=True)]
    ppermute x4 -> x2, starting transfers between devices: 9.52 us -> 7.5 us  [from_behind(): return lax.ppermute(x, axis, [(i, (i + by) % count) for i in range(count)])]
  transfers between devices with their start and end apart: 4 -> 3, of which waited for: 0 -> 1; matrix products, arithmetic and copies ran while one was open for 49% -> 61% of each run, Pallas kernels for 0% -> 0%
where the time goes in v1:
time: 127 us
  matrix products  89.8 us (71%)
  starting transfers between devices  10 us (8%)
  waiting for transfers between devices  7.1 us (6%)
  blocking collectives  7.02 us (6%)
  other arithmetic  5.89 us (5%)
  local copies, waits for them, and re-layouts  3.87 us (3%)
  between operations  3.14 us (2%)
    dot_general x1, matrix products, absorb(): jnp.einsum('xmvbdrp,vmesp->xbdres', second, masked_ket, preferred_element...  38.6 us
    dot_general x1, matrix products, absorb(): jnp.einsum('xlmuvb,uldrp->xmvbdrp', first, masked_ket, preferred_element_...  28.1 us
    dot_general x1, matrix products, absorb(): jnp.einsum('xbdres,brsy->xdey', third, masked_right, preferred_element_ty...  17.4 us
    ppermute x2, starting transfers between devices, from_behind(): return lax.ppermute(x, axis, [(i, (i + by) % count) for i in range(count)])  7.5 us
    all_to_all x1, waiting for transfers between devices, local(): incoming = lax.all_to_all(outgoing, ('col', 'sec'), 0, 0, tiled=True)  7.1 us
    dot_general x1, matrix products, absorb(): jnp.einsum('xalm,auvb->xlmuvb', masked_left, masked_mps, preferred_elemen...  5.8 us
    all_gather x1, blocking collectives, local(): full_mps = lax.all_gather(mps, 'sec', axis=1, tiled=True)  4.2 us
    all_gather x1, blocking collectives, local(): right_next = lax.all_gather(partial_next, 'sec', axis=4, tiled=True)  2.82 us
  transfers between devices with their start and end apart: 3, of which 1 were waited for; matrix products, arithmetic and copies ran while one was open for 61% of the time, Pallas kernels for 0%

profile of v1, /device:TPU:0, one launch (start us, length us, event | category | flops | bytes accessed | tf_op | source)
XLA Modules:
  0.0 126.8 jit_solution(2410546916733743179)
XLA Ops:
  0.6 0.8 pad_add_fusion
  1.4 7.0 %collective-permute-start = (s32[1,198]{1,0:T(1,128)S(1)}, s32[1,198]{1,0:T(1,128)S(1)}, u32[]{:S(2)}, u32[]{:S(2)}) collective-permute-start(s32[1,198]{1,0:T(1,128)S(1)} %pad_add_fusion), channel_id=1, source_target_pairs={{0,30},{2,0},{4,2},{6,4},{8,6},{10,8},{12,10},{14,12},{16,14},{18,... | collective-permute-start | bytes 2384 | tf_op jit(solution)/shard_map/ppermute | solution.py:9
  8.4 0.5 collective-permute-start.1
  8.9 0.8 slice_bitcast_fusion.3
  9.6 0.7 broadcast_add_fusion.2
  10.4 0.7 broadcast_add_fusion.4
  11.1 4.2 %all_gather.6 = bf16[1,96,6,6,96]{4,1,3,2,0:T(8,128)(2,1)} all-gather(bf16[1,48,6,6,96]{4,1,3,2,0:T(8,128)(2,1)} %param.8), channel_id=1, replica_groups=mesh['col'=16,'sec'=2] {'sec'}, dimensions={1}, use_global_device_ids=true | all-gather | bytes 995328 | tf_op jit(solution)/shard_map/all_gather | solution.py:69
  15.3 0.7 broadcast_subtract_fusion.1
  16.0 0.7 dynamic-slice_bitcast_fusion
  16.9 1.1 fusion.30
  18.1 5.8 %convert_bitcast_fusion = bf16[48,6,6,6,6,96,1,1]{5,0,4,3,2,1,7,6:T(8,128)(2,1)S(1)} fusion(bf16[1,96,6,6,96]{4,1,3,2,0:T(8,128)(2,1)} %all_gather.6, s32[96]{0:T(128)S(1)} %get-tuple-element.3, s32[96,6,6]{0,2,1:T(8,128)S(1)} %get-tuple-element.12, bf16[1,48,96,6,6]{2,1,4,3,0:T(8,128)(2,1)} %param.10, s32[96,6,6]{0,2,1:T(8,128)S(1)} %get-tuple-element.13, ...), kind=kOutput, calls=%fused_computation.8 | convolution fusion | flops 1153585152 | bytes 12967488 | tf_op jit(solution)/shard_map/xalm,auvb->xlmuvb/dot_general | solution.py:54
  23.9 28.1 %fusion = bf16[48,6,6,96,6,6,2,1]{3,5,6,4,2,1,0,7:T(8,128)(2,1)} fusion(bf16[48,6,6,6,6,96,1,1]{5,0,4,3,2,1,7,6:T(8,128)(2,1)S(1)} %convert_bitcast_fusion, bf16[6,6,6,6,2,1,1,1]{3,4,2,1,0,7,6,5:T(2,128)(2,1)S(1)} %fusion.30), kind=kOutput, calls=%fused_computation.1 | convolution fusion | flops 871907328 | bytes 35836992 | tf_op jit(solution)/shard_map/xlmuvb,uldrp->xmvbdrp/dot_general | solution.py:57
  52.0 38.6 %bitcast_convert_fusion.1 = bf16[48,96,6,6,6,6]{1,5,4,3,2,0:T(8,128)(2,1)} fusion(bf16[48,6,6,96,6,6,2,1]{3,5,6,4,2,1,0,7:T(8,128)(2,1)} %fusion, bf16[6,6,6,6,2,1,1,1]{3,4,2,1,0,7,6,5:T(2,128)(2,1)S(1)} %fusion.30), kind=kOutput, calls=%fused_computation.2 | convolution fusion | flops 865935360 | bytes 35836992 | tf_op jit(solution)/shard_map/xmvbdrp,vmesp->xbdres/dot_general | solution.py:60
  90.7 2.8 %all_gather.7 = bf16[1,96,6,6,96]{1,4,3,2,0:T(8,128)(2,1)S(1)} all-gather(bf16[1,96,6,6,48]{1,4,3,2,0:T(8,128)(2,1)} %collective-permute-done.1), channel_id=1, replica_groups=mesh['col'=16,'sec'=2] {'sec'}, dimensions={4}, use_global_device_ids=true | all-gather | bytes 995328 | tf_op jit(solution)/shard_map/all_gather | solution.py:81
  93.5 17.4 %multiply_reduce_fusion = (f32[]{:T(128)}, f32[48,6,6,96]{3,0,2,1:T(8,128)S(1)}) fusion(bf16[1,96,6,6,96]{1,4,3,2,0:T(8,128)(2,1)S(1)} %all_gather.7, s32[96,6,6]{0,2,1:T(8,128)S(1)} %broadcast_subtract_fusion, s32[96]{0:T(128)S(1)} %get-tuple-element.2, bf16[48,96,6,6,6,6]{1,5,4,3,2,0:T(8,128)(2,1)} %bitcast_convert_fusion.1), kind=kOutput, calls=%fused_computation.16 | convolution fusion | flops 1147613184 | bytes 13285252 | tf_op jit(solution)/shard_map/xbdres,brsy->xdey/dot_general | solution.py:63
  110.9 1.3 broadcast_in_dim.14
  112.2 2.5 %all-to-all-start = ((f32[32,1,128]{2,1,0:T(1,128)}), f32[32,1,128]{2,1,0:T(1,128)S(1)}, u32[]{:S(2)}, u32[]{:S(2)}) async-start(f32[32,1,128]{2,1,0:T(1,128)} %broadcast_in_dim.14), calls=%async_computation | async-start | bytes 32768 | tf_op jit(solution)/shard_map/all_to_all | solution.py:105
  114.7 7.1 %all-to-all-done = f32[32,1,128]{2,1,0:T(1,128)S(1)} async-done(((f32[32,1,128]{2,1,0:T(1,128)}), f32[32,1,128]{2,1,0:T(1,128)S(1)}, u32[]{:S(2)}, u32[]{:S(2)}) %all-to-all-start) | async-done | bytes 16416 | tf_op jit(solution)/shard_map/all_to_all | solution.py:105
  121.8 0.3 slice_reduce_fusion
  122.1 0.1 reshape_squeeze.3
  122.2 0.1 reduce_sum.28
  122.3 0.6 multiply_reduce_fusion.1
  123.0 0.6 dynamic_slice.7
  124.2 0.8 fusion.22
  (8 shorter events, 0.4 us)
Async XLA Ops:
  1.4 15.4 %collective-permute-start = (s32[1,198]{1,0:T(1,128)S(1)}, s32[1,198]{1,0:T(1,128)S(1)}, u32[]{:S(2)}, u32[]{:S(2)}) collective-permute-start(s32[1,198]{1,0:T(1,128)S(1)} %pad_add_fusion), channel_id=1, source_target_pairs={{0,30},{2,0},{4,2},{6,4},{8,6},{10,8},{12,10},{14,12},{16,14},{18,... | collective-permute-start | bytes 2384 | tf_op jit(solution)/shard_map/ppermute | solution.py:9
  8.4 82.4 %collective-permute-start.1 = (bf16[1,96,6,6,48]{1,4,3,2,0:T(8,128)(2,1)}, bf16[1,96,6,6,48]{1,4,3,2,0:T(8,128)(2,1)}, u32[]{:S(2)}, u32[]{:S(2)}) collective-permute-start(bf16[1,96,6,6,48]{1,4,3,2,0:T(8,128)(2,1)} %param.11), channel_id=1, source_target_pairs={{0,30},{2,0},{4,2},{6,4},{8,6},{10,8},{12,10},{14,12},{16,14},{18,... | collective-permute-start | bytes 995336 | tf_op jit(solution)/shard_map/ppermute | solution.py:9
  112.2 9.7 %all-to-all-start = ((f32[32,1,128]{2,1,0:T(1,128)}), f32[32,1,128]{2,1,0:T(1,128)S(1)}, u32[]{:S(2)}, u32[]{:S(2)}) async-start(f32[32,1,128]{2,1,0:T(1,128)} %broadcast_in_dim.14), calls=%async_computation | async-start | bytes 32768 | tf_op jit(solution)/shard_map/all_to_all | solution.py:105

commit v2 on v1

v2 whole, which is shorter than its diff:
```python
import functools

import jax
import jax.numpy as jnp
import numpy as np
from jax import lax
from jax.experimental import pallas as pl
from jax.experimental.pallas import tpu as pltpu
from jax.sharding import PartitionSpec as P

LANES = 128
XBLOCK = 8


def round_up(value, multiple):
    return -(-value // multiple) * multiple


def from_behind(x, axis, by):
    count = lax.axis_size(axis)
    return lax.ppermute(x, axis, [(i, (i + by) % count) for i in range(count)])


class Plan:
    def __init__(self, chi, half, legs, phys):
        self.chi, self.half, self.legs, self.phys = chi, half, legs, phys
        self.lanes = round_up(chi, LANES)
        self.lm = round_up(legs * legs, 8)
        self.pairs = legs // 2
        self.group_rows = 2 * legs * phys
        self.groups = legs * self.pairs
        self.rows2 = self.groups * self.group_rows
        self.cols2 = round_up(legs * self.lm, 256)
        self.seg = round_up(2 * legs, 16)
        self.rows3 = legs * self.seg
        self.cols3 = legs * self.group_rows
        self.xrows = self.pairs * self.seg

    def matrices(self):
        n, ph = self.legs, self.phys
        r2 = np.zeros((self.rows2, n * n * ph), np.float32)
        c2 = np.zeros((n * n, self.cols2), np.float32)
        m2 = np.zeros((self.rows2, self.cols2), np.float32)
        col_m = np.full((self.cols2,), -1)
        for u in range(n):
            for l in range(n):
                for m in range(n):
                    c = u * self.lm + l * n + m
                    c2[u * n + l, c] = 1
                    col_m[c] = m
        row_m = np.zeros((self.rows2,), np.int64)
        for r in range(n):
            for d in range(n):
                for m in range(n):
                    for p in range(ph):
                        g = r * self.pairs + d // 2
                        row = g * self.group_rows + (d % 2) * n * ph + m * ph + p
                        r2[row, (d * n + r) * ph + p] = 1
                        row_m[row] = m
        m2[:] = row_m[:, None] == col_m[None, :]
        r3 = np.zeros((self.rows3, n * n), np.float32)
        c3 = np.zeros((n * n * ph, self.cols3), np.float32)
        row_d = np.full((self.rows3,), -1)
        for s in range(n):
            for d2 in range(2):
                for e in range(n):
                    row = s * self.seg + d2 * n + e
                    r3[row, e * n + s] = 1
                    row_d[row] = d2
        col_d = np.zeros((self.cols3,), np.int64)
        for v in range(n):
            for d2 in range(2):
                for m in range(n):
                    for p in range(ph):
                        col = v * self.group_rows + d2 * n * ph + m * ph + p
                        c3[(v * n + m) * ph + p, col] = 1
                        col_d[col] = d2
        m3 = (row_d[:, None] == col_d[None, :]).astype(np.float32)
        as_bf16 = lambda x: jnp.asarray(x, jnp.bfloat16)
        return [as_bf16(x) for x in (r2, c2, m2, r3, c3, m3)]

    def indices(self):
        n, ph = self.legs, self.phys
        count = n * n * ph
        rows = np.zeros((count, 8), np.int32)
        cols = np.zeros((8, count), np.int32)
        for i in range(count):
            hi, mid, p = i // (n * ph), (i // ph) % n, i % ph
            rows[i, :3] = hi, mid, p
            cols[:3, i] = hi, mid, p
            if i < n * n:
                rows[i, 3:5] = i // n, i % n
                cols[3:5, i] = i // n, i % n
        return jnp.asarray(rows), jnp.asarray(cols)


def look_up(index, table):
    out = jnp.zeros(index.shape, jnp.int32)
    for k, value in enumerate(table):
        out = out + jnp.where(index == k, value, 0)
    return out


def dot(a, b):
    return jnp.dot(a, b, preferred_element_type=jnp.float32)


def absorb_kernel(
    plan,
    next_s,
    own_s,
    next_v,
    bond_col,
    mine,
    other,
    lhs,
    ket_a,
    ket_b,
    r2,
    c2,
    m2,
    r3,
    c3,
    m3,
    rows,
    cols,
    pr_mine,
    pr_other,
    image,
    partial,
    ms,
    k2,
    k3,
    pr,
    w1,
    w2,
    w3,
):
    n, ph, chi, half = plan.legs, plan.phys, plan.chi, plan.half
    lanes, lm, gr = plan.lanes, plan.lm, plan.group_rows
    step = pl.program_id(0)
    bf16 = jnp.bfloat16

    @pl.when(step == 0)
    def _():
        sec = lax.axis_index("sec")
        link = [own_s[0, i] for i in range(n)]
        upper = [own_s[0, n + i] for i in range(n)]
        lower = [own_s[0, 2 * n + i] for i in range(n)]
        link_next = [next_s[0, 2 * chi + i] for i in range(n)]
        bond_next = next_v[:, :chi]
        ms[...] = jnp.zeros_like(ms)
        for k, src in enumerate((mine, other)):
            which = sec if k == 0 else 1 - sec
            at = pl.multiple_of(which * half, 16)
            gap = bond_next - bond_col[pl.ds(at, half), :]
            for u in range(n):
                for v in range(n):
                    keep = gap == upper[u] - upper[v]
                    val = jnp.where(keep, src[u * n + v].astype(jnp.float32), 0.0)
                    ms[u, v // 2, pl.ds(at, half), (v % 2) * lanes : (v % 2) * lanes + chi] = val.astype(bf16)
        row_a = look_up(rows[:, 0:1], lower) + look_up(rows[:, 1:2], link_next) + rows[:, 2:3]
        col_a = look_up(cols[3:4, : n * n], upper) + look_up(cols[4:5, : n * n], link)
        kept_a = jnp.where(row_a == col_a, ket_a[...].astype(jnp.float32), 0.0).astype(bf16)
        wide = dot(dot(r2[...], kept_a).astype(bf16), c2[...])
        k2[...] = (wide * m2[...].astype(jnp.float32)).astype(bf16)
        row_b = look_up(rows[: n * n, 3:4], lower) + look_up(rows[: n * n, 4:5], link_next)
        col_b = look_up(cols[0:1, :], upper) + look_up(cols[1:2, :], link) - cols[2:3, :]
        kept_b = jnp.where(row_b == col_b, ket_b[...].astype(jnp.float32), 0.0).astype(bf16)
        wide = dot(dot(r3[...], kept_b).astype(bf16), c3[...])
        k3[...] = (wide * m3[...].astype(jnp.float32)).astype(bf16)
        square = (chi, chi)
        diagonal = lax.broadcasted_iota(jnp.int32, square, 0) == lax.broadcasted_iota(jnp.int32, square, 1)
        fresh_row = jnp.broadcast_to(next_v[:, chi : 2 * chi], square)
        fresh_col = jnp.sum(jnp.where(diagonal, fresh_row, 0), axis=1, keepdims=True)
        gap_low = fresh_col[:half] - bond_next
        gap_high = fresh_col[half:] - bond_next
        pr[...] = jnp.zeros_like(pr)
        for k, src in enumerate((pr_mine, pr_other)):
            which = sec if k == 0 else 1 - sec
            at = pl.multiple_of(which * half, 16)
            gap = jnp.where(which == 0, gap_low, gap_high)
            for r in range(n):
                for s in range(n):
                    keep = gap == link_next[r] - link_next[s]
                    val = jnp.where(keep, src[r * n + s].astype(jnp.float32), 0.0)
                    pr[r, pl.ds(at, half), s * lanes : s * lanes + chi] = val.astype(bf16)
        w1[...] = jnp.zeros_like(w1)
        partial[...] = jnp.zeros_like(partial)

    for q in range(XBLOCK // 2):
        slot = q % 2
        left = lhs[q * 2 * lm : (q + 1) * 2 * lm, :]
        for vp in range(plan.pairs):
            for up in range(plan.pairs):
                lo = dot(left, ms[2 * up, vp])
                hi = dot(left, ms[2 * up + 1, vp])
                for x in range(2):
                    both = jnp.concatenate([lo[x * lm : (x + 1) * lm], hi[x * lm : (x + 1) * lm]], axis=0)
                    w1[slot, x, vp, up * 2 * lm : (up + 1) * 2 * lm, :] = both.astype(bf16)
            for x in range(2):
                out = dot(k2[...], w1[slot, x, vp])
                for g in range(plan.groups):
                    part = out[g * gr : (g + 1) * gr]
                    both = jnp.concatenate([part[:, :lanes], part[:, lanes:]], axis=0)
                    w2[slot, g, vp * 2 * gr : (vp + 1) * 2 * gr, x * lanes : (x + 1) * lanes] = both.astype(bf16)
        for g in range(plan.groups):
            r, dp = g // plan.pairs, g % plan.pairs
            out = dot(k3[...], w2[slot, g]).astype(bf16)
            for s in range(n):
                for x in range(2):
                    at = (q * 2 + x) * plan.xrows + dp * plan.seg
                    w3[r, at : at + plan.seg, s * lanes : (s + 1) * lanes] = out[
                        s * plan.seg : (s + 1) * plan.seg, x * lanes : (x + 1) * lanes
                    ]
    total = None
    for r in range(n):
        term = lax.dot_general(w3[r], pr[r], (((1,), (1,)), ((), ())), preferred_element_type=jnp.float32)
        total = term if total is None else total + term
    image[...] = total
    partial[...] += jnp.sum(total * total)


def absorb(plan, next_all, own_s, bond_col, mine, other, lhs, ket, pr_mine, pr_other):
    n, ph, chi, half = plan.legs, plan.phys, plan.chi, plan.half
    ket_a = jnp.transpose(ket, (2, 3, 4, 0, 1)).reshape(n * n * ph, n * n)
    ket_b = jnp.transpose(ket, (2, 3, 0, 1, 4)).reshape(n * n, n * n * ph)
    steps = half // XBLOCK
    block = XBLOCK * plan.xrows
    operands = [next_all, own_s, next_all, bond_col, mine, other, lhs, ket_a, ket_b]
    operands += plan.matrices() + list(plan.indices()) + [pr_mine, pr_other]
    specs = []
    for i, x in enumerate(operands):
        if i < 2:
            specs.append(pl.BlockSpec(memory_space=pltpu.SMEM))
        elif i == 6:
            specs.append(pl.BlockSpec((XBLOCK * plan.lm, chi), lambda i: (i, 0)))
        else:
            specs.append(pl.BlockSpec(x.shape, functools.partial(lambda nd, i: (0,) * nd, x.ndim)))
    bf16 = jnp.bfloat16
    return pl.pallas_call(
        functools.partial(absorb_kernel, plan),
        grid=(steps,),
        in_specs=specs,
        out_specs=[
            pl.BlockSpec((block, chi), lambda i: (i, 0)),
            pl.BlockSpec((8, LANES), lambda i: (0, 0)),
        ],
        out_shape=[
            jax.ShapeDtypeStruct((half * plan.xrows, chi), jnp.float32),
            jax.ShapeDtypeStruct((8, LANES), jnp.float32),
        ],
        scratch_shapes=[
            pltpu.VMEM((n, plan.pairs, chi, 2 * plan.lanes), bf16),
            pltpu.VMEM((plan.rows2, plan.cols2), bf16),
            pltpu.VMEM((plan.rows3, plan.cols3), bf16),
            pltpu.VMEM((n, chi, n * plan.lanes), bf16),
            pltpu.VMEM((2, 2, plan.pairs, plan.cols2, 2 * plan.lanes), bf16),
            pltpu.VMEM((2, plan.groups, plan.cols3, 2 * plan.lanes), bf16),
            pltpu.VMEM((n, block, n * plan.lanes), bf16),
        ],
        name="absorb",
    )(*operands)


def local(mps, ket, left_proj, right_proj, bond_charge, new_charge, link_charge, vert_charge):
    half, chi, legs = left_proj.shape[1], left_proj.shape[2], left_proj.shape[3]
    phys = ket.shape[5]
    plan = Plan(chi, half, legs, phys)
    columns, sections = lax.axis_size("col"), lax.axis_size("sec")
    swap = [(i, 1 - i) for i in range(sections)]
    packed = jnp.concatenate([bond_charge, new_charge, link_charge], axis=1)
    next_all = from_behind(packed, "col", -1)
    mine = jnp.transpose(mps[0], (1, 2, 0, 3)).reshape(legs * legs, half, chi)
    other = lax.ppermute(mine, "sec", swap)
    pr_mine = from_behind(jnp.transpose(right_proj[0], (1, 2, 3, 0)).reshape(legs * legs, half, chi), "col", -1)
    pr_other = lax.ppermute(pr_mine, "sec", swap)
    sec = lax.axis_index("sec")
    fresh = lax.dynamic_slice_in_dim(new_charge[0], sec * half, half, 0)
    link = link_charge[0]
    keep = (
        fresh[None, None, :, None]
        == bond_charge[0][None, None, None, :] + link[:, None, None, None] - link[None, :, None, None]
    )
    left = jnp.transpose(left_proj[0], (2, 3, 0, 1))
    left = jnp.where(keep, left, jnp.zeros_like(left)).reshape(legs * legs, half, chi)
    left = jnp.transpose(left, (1, 0, 2))
    left = jnp.pad(left, ((0, 0), (0, plan.lm - legs * legs), (0, 0))).reshape(half * plan.lm, chi)
    own_s = jnp.concatenate([link_charge, vert_charge[:, 0], vert_charge[:, 1]], axis=1)
    image, partial = absorb(
        plan, next_all, own_s, bond_charge[0][:, None], mine, other, left, ket[0], pr_mine, pr_other
    )
    count = chi * legs * legs * chi
    outgoing = jnp.broadcast_to(partial[:1], (columns * sections, 1, LANES))
    incoming = lax.all_to_all(outgoing, ("col", "sec"), 0, 0, tiled=True)
    squares = jnp.sum(incoming[:, 0, 0].reshape(columns, sections), axis=1)
    meansq_all = squares / count
    log_norm = jnp.sum(0.5 * jnp.log(meansq_all + 1e-06)) / columns
    meansq = lax.dynamic_slice_in_dim(meansq_all, lax.axis_index("col"), 1, 0)
    scale = lax.rsqrt(meansq + 1e-06)[0]
    shaped = image.reshape(half, plan.pairs, plan.seg, chi)[:, :, : 2 * legs].reshape(half, legs, legs, chi)
    new_mps = (shaped * scale).astype(jnp.bfloat16)[None]
    return (new_mps, log_norm)


def solution(mesh):
    placed = (
        P("col", "sec", None, None, None),
        P("col", None, None, None, None, None),
        P("col", "sec", None, None, None),
        P("col", None, None, None, "sec"),
        P("col", None),
        P("col", None),
        P("col", None),
        P("col", None, None),
    )
    return jax.shard_map(
        local,
        mesh=mesh,
        in_specs=placed,
        out_specs=(P("col", "sec", None, None, None), P()),
        check_vma=False,
    )
```

time: 127 us -> 99.6 us (0.78)
  matrix products: 89.8 us -> 0 us
  Pallas kernels: 0 us -> 49.9 us
  waiting for transfers between devices: 7.1 us -> 16 us
  blocking collectives: 7.02 us -> 0 us
  local copies, waits for them, and re-layouts: 3.87 us -> 10.3 us
  starting transfers between devices: 10 us -> 12.1 us
  other arithmetic: 5.89 us -> 7.75 us
    dot_general x4 -> x0, matrix products: 89.8 us -> none  [the longest x1 38.6 us: absorb(): jnp.einsum('xmvbdrp,vmesp->xbdres', second, masked_ket, preferred_element...]
    pallas_call x0 -> x1, Pallas kernels: none -> 49.9 us  [absorb(): pl.pallas_call(functools.partial(absorb_kernel, plan), grid=(steps,), in_...]
    ppermute x2, waiting for transfers between devices: 0.01 us -> 8.88 us  [from_behind(): return lax.ppermute(x, axis, [(i, (i + by) % count) for i in range(count)])]
    all_gather x2 -> x0, blocking collectives: 7.02 us -> none  [the longest x1 4.2 us: local(): full_mps = lax.all_gather(mps, 'sec', axis=1, tiled=True)]
    all_to_all x1, starting transfers between devices: 2.54 us -> 4.61 us  [local(): incoming = lax.all_to_all(outgoing, ('col', 'sec'), 0, 0, tiled=True)]
    reshape x0 -> x4, local copies, waits for them, and re-layouts: none -> 1.7 us  [the longest x2 0.83 us: absorb(): ket_b = jnp.transpose(ket, (2, 3, 0, 1, 4)).reshape(n * n, n * n * ph)]
    transpose x0 -> x2, local copies, waits for them, and re-layouts: none -> 1.66 us  [the longest x1 0.92 us: absorb(): ket_b = jnp.transpose(ket, (2, 3, 0, 1, 4)).reshape(n * n, n * n * ph)]
    convert_element_type x1, other arithmetic: 0.83 us -> 2.32 us  [local(): new_mps = (shaped * scale).astype(jnp.bfloat16)[None]]
  transfers between devices with their start and end apart: 3 -> 5, of which waited for: 1 -> 2; matrix products, arithmetic and copies ran while one was open for 61% -> 11% of each run, Pallas kernels for 0% -> 0%
where the time goes in v2:
time: 99.6 us; the launch traced here: 99.2 us
  Pallas kernels  49.9 us (50%)
  waiting for transfers between devices  16 us (16%)
  starting transfers between devices  12.1 us (12%)
  local copies, waits for them, and re-layouts  10.3 us (10%)
  other arithmetic  7.75 us (8%)
  between operations  3.19 us (3%)
    pallas_call x1, Pallas kernels, absorb(): pl.pallas_call(functools.partial(absorb_kernel, plan), grid=(steps,), in_...  49.9 us
    ppermute x2, waiting for transfers between devices, from_behind(): return lax.ppermute(x, axis, [(i, (i + by) % count) for i in range(count)])  8.88 us
    ppermute x2, starting transfers between devices, from_behind(): return lax.ppermute(x, axis, [(i, (i + by) % count) for i in range(count)])  7.5 us
    all_to_all x1, waiting for transfers between devices, local(): incoming = lax.all_to_all(outgoing, ('col', 'sec'), 0, 0, tiled=True)  7.1 us
    all_to_all x1, starting transfers between devices, local(): incoming = lax.all_to_all(outgoing, ('col', 'sec'), 0, 0, tiled=True)  4.61 us
    convert_element_type x1, other arithmetic, local(): new_mps = (shaped * scale).astype(jnp.bfloat16)[None]  2.32 us
  transfers between devices with their start and end apart: 5, of which 2 were waited for; matrix products, arithmetic and copies ran while one was open for 11% of the time, Pallas kernels for 0%

profile of v2, /device:TPU:0, one launch (start us, length us, event | category | flops | bytes accessed | tf_op | source)
XLA Modules:
  0.0 99.2 jit_solution(7695456442252144391)
XLA Ops:
  0.6 0.8 pad_add_fusion
  1.4 7.0 %collective-permute-start = (s32[1,198]{1,0:T(1,128)S(1)}, s32[1,198]{1,0:T(1,128)S(1)}, u32[]{:S(2)}, u32[]{:S(2)}) collective-permute-start(s32[1,198]{1,0:T(1,128)S(1)} %pad_add_fusion), channel_id=1, source_target_pairs={{0,30},{2,0},{4,2},{6,4},{8,6},{10,8},{12,10},{14,12},{16,14},{18,... | collective-permute-start | bytes 2384 | tf_op jit(solution)/shard_map/ppermute | solution.py:21
  8.9 0.7 broadcast_add_fusion
  9.7 0.7 broadcast_subtract_fusion
  10.4 0.7 dynamic-slice_bitcast_fusion
  11.1 1.2 %compare_select_fusion = bf16[6,6,48,96]{3,2,1,0:T(8,128)(2,1)S(1)} fusion(bf16[1,48,96,6,6]{2,1,4,3,0:T(8,128)(2,1)} %param.18, s32[6,6,96]{2,1,0:T(8,128)S(1)} %broadcast_subtract_fusion, s32[48]{0:T(128)S(1)} %dynamic-slice_bitcast_fusion), kind=kLoop, calls=%fused_computation.2 | loop fusion | flops 331776 | bytes 677568 | tf_op jit(solution)/shard_map/jit(_where)/select_n | solution.py:286
  12.3 8.9 %collective-permute-done.2.pr_mine = bf16[36,48,96]{2,1,0:T(8,128)(2,1)S(1)} collective-permute-done((bf16[36,48,96]{2,1,0:T(8,128)(2,1)}, bf16[36,48,96]{2,1,0:T(8,128)(2,1)S(1)}, u32[]{:S(2)}, u32[]{:S(2)}) %collective-permute-start.2) | collective-permute-done | bytes 331808 | tf_op jit(solution)/shard_map/ppermute | solution.py:21
  21.2 0.8 slice_bitcast_fusion.2
  22.0 1.2 %pad_add_fusion.1.own_s = s32[1,18]{1,0:T(1,128)} fusion(s32[1,6]{1,0:T(1,128)S(1)} %get-tuple-element.7, s32[1,6]{1,0:T(1,128)S(1)} %get-tuple-element.6, s32[1,6]{1,0:T(1,128)} %param.22), kind=kLoop, calls=%fused_computation.8 | loop fusion | flops 36 | bytes 144 | tf_op jit(solution)/shard_map/concatenate | solution.py:289
  23.2 1.4 %copy.38.bond_col = s32[96,1]{1,0:T(8,128)} copy(s32[96,1]{0,1:T(1,128)} %bitcast.53) | data formatting | bytes 768 | tf_op jit(solution)/shard_map/broadcast_in_dim;squeeze | solution.py:291
  24.6 0.9 copy.37
  25.6 0.7 copy.39.ket_b
  26.3 0.7 copy.36
  27.1 0.8 reshape.89.ket_a
  27.9 0.9 pad.4
  28.9 0.5 copy-done.4
  29.8 49.9 %absorb.1 = (f32[2304,96]{1,0:T(8,128)}, f32[8,128]{1,0:T(8,128)}) custom-call(s32[1,198]{1,0:T(1,128)} %copy-done.4, s32[1,18]{1,0:T(1,128)} %pad_add_fusion.1.own_s, s32[1,198]{1,0:T(1,128)} %copy-done.4, s32[96,1]{1,0:T(8,128)} %copy.38.bond_col, bf16[36,48,96]{2,1,0:T(8,128)(2,1)} %bitcast.49, bf16[36,48,96]{2,1,0:T(8,128)(2,1)} %copy-done.1, ...), custom_call_target="tpu_custom_call" | custom-call | tf_op jit(solution)/shard_map/absorb/pallas_call | solution.py:241
  79.7 0.7 slice_bitcast_fusion
  80.4 0.6 broadcast_in_dim.9
  81.0 4.6 %all-to-all-start = ((f32[32,1,128]{2,1,0:T(1,128)}), f32[32,1,128]{2,1,0:T(1,128)S(1)}, u32[]{:S(2)}, u32[]{:S(2)}) async-start(f32[32,1,128]{2,1,0:T(1,128)} %broadcast_in_dim.9), calls=%async_computation | async-start | bytes 32768 | tf_op jit(solution)/shard_map/all_to_all | solution.py:295
  85.6 7.1 %all-to-all-done = f32[32,1,128]{2,1,0:T(1,128)S(1)} async-done(((f32[32,1,128]{2,1,0:T(1,128)}), f32[32,1,128]{2,1,0:T(1,128)S(1)}, u32[]{:S(2)}, u32[]{:S(2)}) %all-to-all-start) | async-done | bytes 16416 | tf_op jit(solution)/shard_map/all_to_all | solution.py:295
  93.2 0.6 multiply_reduce_fusion
  93.8 0.6 dynamic_slice.7
  95.8 2.3 %fusion = bf16[48,3,12,96]{3,0,2,1:T(8,128)(2,1)} fusion(f32[48,3,12,96]{3,2,1,0:T(8,128)} %bitcast.44, f32[]{:T(128)} %bitcast.24), kind=kLoop, calls=%fused_computation.1 | loop fusion | flops 331776 | bytes 995332 | tf_op jit(solution)/shard_map/convert_element_type | solution.py:302
  (20 shorter events, 1.7 us)
Async XLA Ops:
  0.6 25.7 %copy-start = (bf16[1,6,6,6,6,2]{4,5,3,2,1,0:T(2,128)(2,1)S(1)}, bf16[1,6,6,6,6,2]{4,5,3,2,1,0:T(2,128)(2,1)}, u32[]{:S(2)}) copy-start(bf16[1,6,6,6,6,2]{4,5,3,2,1,0:T(2,128)(2,1)} %param.17) | copy-start | bytes 15556
  1.4 27.4 %collective-permute-start = (s32[1,198]{1,0:T(1,128)S(1)}, s32[1,198]{1,0:T(1,128)S(1)}, u32[]{:S(2)}, u32[]{:S(2)}) collective-permute-start(s32[1,198]{1,0:T(1,128)S(1)} %pad_add_fusion), channel_id=1, source_target_pairs={{0,30},{2,0},{4,2},{6,4},{8,6},{10,8},{12,10},{14,12},{16,14},{18,... | collective-permute-start | bytes 2384 | tf_op jit(solution)/shard_map/ppermute | solution.py:21
  8.4 20.5 %collective-permute-start.1 = (bf16[36,48,96]{2,1,0:T(8,128)(2,1)}, bf16[36,48,96]{2,1,0:T(8,128)(2,1)S(1)}, u32[]{:S(2)}, u32[]{:S(2)}) collective-permute-start(bf16[36,48,96]{2,1,0:T(8,128)(2,1)} %bitcast.48), channel_id=1, source_target_pairs={{0,1},{1,0},{2,3},{3,2},{4,5},{5,4},{6,7},{7,6},{8,9},{9,8},{10,11... | collective-permute-start | bytes 995336 | tf_op jit(solution)/shard_map/ppermute | solution.py:275
  8.4 12.8 %collective-permute-start.2 = (bf16[36,48,96]{2,1,0:T(8,128)(2,1)}, bf16[36,48,96]{2,1,0:T(8,128)(2,1)S(1)}, u32[]{:S(2)}, u32[]{:S(2)}) collective-permute-start(bf16[36,48,96]{2,1,0:T(8,128)(2,1)} %bitcast.54), channel_id=1, source_target_pairs={{0,30},{2,0},{4,2},{6,4},{8,6},{10,8},{12,10},{14,12},{16,14},{18,... | collective-permute-start | bytes 995336 | tf_op jit(solution)/shard_map/ppermute | solution.py:21
  21.2 7.7 %copy-start.2 = (bf16[36,48,96]{2,1,0:T(8,128)(2,1)}, bf16[36,48,96]{2,1,0:T(8,128)(2,1)S(1)}, u32[]{:S(2)}) copy-start(bf16[36,48,96]{2,1,0:T(8,128)(2,1)S(1)} %collective-permute-done.2.pr_mine) | copy-start | bytes 995332
  21.2 7.7 %collective-permute-start.3 = (bf16[36,48,96]{2,1,0:T(8,128)(2,1)S(1)}, bf16[36,48,96]{2,1,0:T(8,128)(2,1)S(1)}, u32[]{:S(2)}, u32[]{:S(2)}) collective-permute-start(bf16[36,48,96]{2,1,0:T(8,128)(2,1)S(1)} %collective-permute-done.2.pr_mine), channel_id=1, source_target_pairs={{0,1},{1,0},{2,3},{3,2},{4,5},{5,4},{6,7},{7,6},{8,9},{9,8},{10,11... | collective-permute-start | bytes 995336 | tf_op jit(solution)/shard_map/ppermute | solution.py:277
  28.9 0.6 copy-start.4
  28.9 0.8 copy-start.1
  28.9 0.9 copy-start.3
  81.0 11.7 %all-to-all-start = ((f32[32,1,128]{2,1,0:T(1,128)}), f32[32,1,128]{2,1,0:T(1,128)S(1)}, u32[]{:S(2)}, u32[]{:S(2)}) async-start(f32[32,1,128]{2,1,0:T(1,128)} %broadcast_in_dim.9), calls=%async_computation | async-start | bytes 32768 | tf_op jit(solution)/shard_map/all_to_all | solution.py:295

commit v3 on v0

v3 whole, which is shorter than its diff:
```python
import functools

import jax
import jax.numpy as jnp
import numpy as np
from jax import lax
from jax.experimental import pallas as pl
from jax.experimental.pallas import tpu as pltpu
from jax.sharding import PartitionSpec as P

LANES = 128
QUAD = 4
VMEM_LIMIT = 36 << 20
FRONT_FLOPS = 1 << 30


def round_up(value, multiple):
    return -(-value // multiple) * multiple


def from_behind(x, axis, by):
    count = lax.axis_size(axis)
    return lax.ppermute(x, axis, [(i, (i + by) % count) for i in range(count)])


class Plan:
    def __init__(self, chi, half, legs, phys):
        self.chi, self.half, self.legs, self.phys = chi, half, legs, phys
        self.lanes = round_up(chi, LANES)
        self.lm = round_up(legs * legs, 8)
        self.pairs = legs // 2
        self.group_rows = 2 * legs * phys
        self.groups = legs * self.pairs
        self.rows2 = self.groups * self.group_rows
        self.cols2 = round_up(legs * self.lm, 256)
        self.seg = round_up(2 * legs, 16)
        self.rows3 = legs * self.seg
        self.cols3 = legs * self.group_rows
        self.xrows = self.pairs * self.seg

    def matrices(self):
        n, ph = self.legs, self.phys
        wide = n * n * ph
        r2 = np.zeros((self.rows2, wide), np.float32)
        row_m = np.zeros((self.rows2,), np.int64)
        for r in range(n):
            for d in range(n):
                for m in range(n):
                    for p in range(ph):
                        g = r * self.pairs + d // 2
                        row = g * self.group_rows + (d % 2) * n * ph + m * ph + p
                        r2[row, (d * ph + p) * n + r] = 1
                        row_m[row] = m
        c2 = np.zeros((n * n, self.cols2), np.float32)
        col_m = np.full((self.cols2,), -1)
        for u in range(n):
            for l in range(n):
                for m in range(n):
                    c = u * self.lm + l * n + m
                    c2[u * n + l, c] = 1
                    col_m[c] = m
        m2 = row_m[:, None] == col_m[None, :]
        r3 = np.zeros((ph, self.rows3, wide), np.float32)
        row_d = np.full((self.rows3,), -1)
        for s in range(n):
            for d2 in range(2):
                for e in range(n):
                    row = s * self.seg + d2 * n + e
                    row_d[row] = d2
                    for p in range(ph):
                        r3[p, row, (e * ph + p) * n + s] = 1
        c3 = np.zeros((ph, n * n, self.cols3), np.float32)
        col_d = np.zeros((self.cols3,), np.int64)
        for v in range(n):
            for d2 in range(2):
                for m in range(n):
                    for p in range(ph):
                        col = v * self.group_rows + d2 * n * ph + m * ph + p
                        c3[p, v * n + m, col] = 1
                        col_d[col] = d2
        m3 = row_d[:, None] == col_d[None, :]
        return [jnp.asarray(x, jnp.bfloat16) for x in (r2, c2, m2, r3, c3, m3)]

    def indices(self):
        n, ph = self.legs, self.phys
        rows = np.zeros((n * n * ph, 8), np.int32)
        cols = np.zeros((8, self.cols2), np.int32)
        for i in range(n * n * ph):
            rest = i % self.group_rows
            rows[i, 0] = i // self.group_rows * 2 + rest // (n * ph)
            rows[i, 1] = rest % ph
        for i in range(self.seg):
            rows[i, 2] = i % n
        for u in range(n):
            for i in range(n * n):
                cols[:2, u * self.lm + i] = u, i // n
        for i in range(self.cols3):
            rest = i % (n * ph)
            cols[2:5, i] = i // self.group_rows, rest // ph, rest % ph
        return [jnp.asarray(rows), jnp.asarray(cols)]


def column_of(row):
    square = (row.shape[1], row.shape[1])
    diagonal = lax.broadcasted_iota(jnp.int32, square, 0) == lax.broadcasted_iota(jnp.int32, square, 1)
    return jnp.sum(jnp.where(diagonal, jnp.broadcast_to(row, square), 0), axis=1, keepdims=True)


def look_up(index, table):
    out = jnp.zeros(index.shape, jnp.int32)
    for k, value in enumerate(table):
        out = out + jnp.where(index == k, value, 0)
    return out


def dot(a, b):
    return jnp.dot(a, b, preferred_element_type=jnp.float32)


def fetch(pairs, sems):
    copies = [pltpu.make_async_copy(src, dst, sems.at[i]) for i, (src, dst) in enumerate(pairs)]
    for copy in copies:
        copy.start()
    return copies


def prep_kernel(
    plan,
    ket, left_h, bond_h, fresh_h, link_h, vert_h, r2_h, c2_h, m2_h, r3_h, c3_h, m3_h, rows_h, cols_h,
    out, k2, k3, gap2, gap3, bond_col,
    wide, left, bond, fresh, link_s, vert_s, r2, c2, m2, r3, c3, m3, rows, cols, sems,
):
    n, half, lm = plan.legs, plan.half, plan.lm
    sources = (link_h, vert_h, bond_h, fresh_h, left_h, r2_h, c2_h, m2_h, r3_h, c3_h, m3_h, rows_h, cols_h)
    targets = (link_s, vert_s, bond, fresh, left, r2, c2, m2, r3, c3, m3, rows, cols)
    copies = fetch(list(zip(sources, targets)), sems)
    for row in range(n * n, lm):
        wide[pl.ds(row, half, stride=lm), :] = jnp.zeros((half, plan.chi), jnp.float32)
    for copy in copies[:5]:
        copy.wait()
    sec = lax.axis_index("sec")
    link = [link_s[0, i] for i in range(n)]
    upper = [vert_s[0, 0, i] for i in range(n)]
    lower = [vert_s[0, 1, i] for i in range(n)]
    fresh_all = column_of(fresh[...])
    fresh_col = jnp.where(sec == 0, fresh_all[:half], fresh_all[half:])
    bond_col[...] = column_of(bond[...])
    gap = fresh_col - bond[...]
    for l in range(n):
        for m in range(n):
            keep = gap == link[l] - link[m]
            val = jnp.where(keep, left[l * n + m].astype(jnp.float32), 0.0)
            wide[pl.ds(l * n + m, half, stride=lm), :] = val
    out[...] = wide[...].astype(jnp.bfloat16)
    for copy in copies[5:]:
        copy.wait()

    def expand(first, second):
        picked = lax.dot_general(first, ket[...], (((1,), (1,)), ((), ())), preferred_element_type=jnp.float32)
        return dot(picked.astype(jnp.bfloat16), second)

    k2[...] = (expand(r2[...], c2[...]) * m2[...].astype(jnp.float32)).astype(jnp.bfloat16)
    total = expand(r3[0], c3[0])
    for p in range(1, plan.phys):
        total = total + expand(r3[p], c3[p])
    k3[...] = (total * m3[...].astype(jnp.float32)).astype(jnp.bfloat16)
    rows_d = look_up(rows[:, 0:1], lower) + rows[:, 1:2]
    gap2[...] = look_up(cols[0:1, :], upper) + look_up(cols[1:2, :], link) - rows_d
    rows_e = look_up(rows[: plan.seg, 2:3], lower)
    c = slice(0, plan.cols3)
    gap3[...] = look_up(cols[2:3, c], upper) + look_up(cols[3:4, c], link) - cols[4:5, c] - rows_e


def halves(first, second):
    sec = lax.axis_index("sec")
    return ((first, sec), (second, 1 - sec))


def first_two(plan, left, ms, k2, w1, w2, vp):
    lanes, lm, gr = plan.lanes, plan.lm, plan.group_rows
    bf16 = jnp.bfloat16
    for up in range(plan.pairs):
        both = dot(left, ms[up, vp])
        for x in range(QUAD):
            part = both[x * lm : (x + 1) * lm]
            stacked = jnp.concatenate([part[:, : 2 * lanes], part[:, 2 * lanes :]], axis=0)
            w1[vp, up * 2 * lm : (up + 1) * 2 * lm, x * 2 * lanes : (x + 1) * 2 * lanes] = stacked.astype(bf16)
    for h in range(QUAD // 2):
        out = dot(k2[...], w1[vp, :, h * 4 * lanes : (h + 1) * 4 * lanes])
        for g in range(plan.groups):
            part = out[g * gr : (g + 1) * gr]
            for j in range(2):
                x = 2 * h + j
                low, high = part[:, 2 * j * lanes : (2 * j + 1) * lanes], part[:, (2 * j + 1) * lanes : (2 * j + 2) * lanes]
                stacked = jnp.concatenate([low, high], axis=0)
                w2[g, vp * 2 * gr : (vp + 1) * 2 * gr, x * lanes : (x + 1) * lanes] = stacked.astype(bf16)


def third(plan, k3, w2, w3, g):
    lanes, seg = plan.lanes, plan.seg
    r, dp = g // plan.pairs, g % plan.pairs
    out = dot(k3[...], w2[g]).astype(jnp.bfloat16)
    for s in range(plan.legs):
        for x in range(QUAD):
            at = x * plan.xrows + dp * seg
            w3[r, at : at + seg, s * lanes : (s + 1) * lanes] = out[s * seg : (s + 1) * seg, x * lanes : (x + 1) * lanes]


def fourth(w3, pr, r):
    return lax.dot_general(w3[r], pr[r], (((1,), (1,)), ((), ())), preferred_element_type=jnp.float32)


def add(total, term):
    return term if total is None else total + term


def quad_rows(lhs, plan, quad):
    rows = QUAD * plan.lm
    return lhs[pl.ds(pl.multiple_of(quad * rows, 16), rows), :]


def front_kernel(
    plan, ahead,
    link_next_s, bond_next_v, other, lhs, k2_all, k3_all, gap2, gap3, bond_col, mine_h, vert_h,
    ms, k2, k3, w3,
    w1, w2, mine, vert_s, sems,
):
    n, chi, half, lanes = plan.legs, plan.chi, plan.half, plan.lanes
    bf16 = jnp.bfloat16
    copies = fetch([(vert_h, vert_s), (mine_h, mine)], sems)
    link_next = [link_next_s[0, i] for i in range(n)]
    tall = plan.pairs * plan.group_rows
    for r in range(n):
        at = slice(r * tall, (r + 1) * tall)
        k2[at] = jnp.where(gap2[...] == link_next[r], k2_all[at].astype(jnp.float32), 0.0).astype(bf16)
        at = slice(r * plan.seg, (r + 1) * plan.seg)
        k3[at] = jnp.where(gap3[...] == link_next[r], k3_all[at].astype(jnp.float32), 0.0).astype(bf16)
    if chi < lanes:
        for k in range(4):
            at = slice(k * lanes + chi, (k + 1) * lanes)
            ms[:, :, :, at] = jnp.zeros((plan.pairs, plan.pairs, chi, lanes - chi), bf16)
    copies[0].wait()
    upper = [vert_s[0, 0, i] for i in range(n)]
    copies[1].wait()
    for src, which in halves(mine, other):
        at = pl.multiple_of(which * half, 16)
        gap = bond_next_v[...] - bond_col[pl.ds(at, half), :]
        for u in range(n):
            for v in range(n):
                keep = gap == upper[u] - upper[v]
                val = jnp.where(keep, src[u * n + v].astype(jnp.float32), 0.0)
                lane = (u % 2 * 2 + v % 2) * lanes
                ms[u // 2, v // 2, pl.ds(at, half), lane : lane + chi] = val.astype(bf16)
    pad = n * plan.lm
    w1[:, :, pad:, :] = jnp.zeros((2, plan.pairs, plan.cols2 - pad, w1.shape[3]), bf16)
    per_g = plan.groups // plan.pairs
    for q in range(ahead + 1):
        for vp in range(plan.pairs):
            if q < ahead:
                first_two(plan, quad_rows(lhs, plan, q), ms, k2, w1.at[q % 2], w2.at[q % 2], vp)
            if q > 0:
                for g in range(vp * per_g, (vp + 1) * per_g):
                    third(plan, k3, w2.at[(q - 1) % 2], w3.at[q - 1], g)


def back_kernel(
    plan, ahead,
    link_next_s,
    bond_next_v, fresh_next_v, lhs, ms, k2, k3, w3_ahead, pr_mine, pr_other,
    image, partial,
    pr, w1, w2, w3,
):
    n, chi, half, lanes = plan.legs, plan.chi, plan.half, plan.lanes
    bf16 = jnp.bfloat16
    link_next = [link_next_s[0, i] for i in range(n)]
    fresh_col = column_of(fresh_next_v[...])
    pr[...] = jnp.zeros_like(pr)
    for src, which in halves(pr_mine, pr_other):
        at = pl.multiple_of(which * half, 16)
        gap = jnp.where(which == 0, fresh_col[:half], fresh_col[half:]) - bond_next_v[...]
        for r in range(n):
            for s in range(n):
                keep = gap == link_next[r] - link_next[s]
                val = jnp.where(keep, src[r * n + s].astype(jnp.float32), 0.0)
                pr[r, pl.ds(at, half), s * lanes : s * lanes + chi] = val.astype(bf16)
    pad = n * plan.lm
    w1[:, :, pad:, :] = jnp.zeros((2, plan.pairs, plan.cols2 - pad, w1.shape[3]), bf16)

    block = QUAD * plan.xrows
    per_g = plan.groups // plan.pairs
    per_r = n // plan.pairs

    def put(quad, total):
        image[pl.ds(pl.multiple_of(quad * block, 8), block), :] = total
        return jnp.sum(total * total)

    def body(step, square_sum):
        early = None
        for k in range(2):
            total = None
            for vp in range(plan.pairs):
                left = quad_rows(lhs, plan, ahead + 2 * step + k)
                first_two(plan, left, ms, k2, w1.at[k], w2.at[k], vp)
                for g in range(vp * per_g, (vp + 1) * per_g):
                    third(plan, k3, w2.at[1 - k], w3.at[1 - k], g)
                for r in range(vp * per_r, (vp + 1) * per_r):
                    total = add(total, fourth(w3.at[k], pr, r))
                    if r % 2 == k:
                        early = add(early, fourth(w3_ahead.at[step], pr, r))
            square_sum = square_sum + jnp.where(step > 0, put(ahead - 2 + 2 * step + k, total), 0.0)
        return square_sum + put(step, early)

    quads = half // QUAD
    steps = (quads - ahead) // 2
    square_sum = lax.fori_loop(0, steps, body, jnp.float32(0.0))
    total = None
    for g in range(plan.groups):
        third(plan, k3, w2.at[1], w3.at[1], g)
        if g % plan.pairs == 0:
            total = add(total, fourth(w3.at[0], pr, g // plan.pairs))
    square_sum = square_sum + put(quads - 2, total)
    even = odd = None
    for r in range(0, n, 2):
        even = add(even, fourth(w3.at[1], pr, r))
        odd = add(odd, fourth(w3.at[1], pr, r + 1))
    square_sum = square_sum + put(quads - 1, even + odd)
    partial[...] = jnp.full_like(partial, square_sum)


def finish_kernel(plan, count, columns, incoming, image, new, log_norm):
    n, half = plan.legs, plan.half
    sums = incoming[...]
    devices = sums.shape[0]
    row = lax.broadcasted_iota(jnp.int32, sums.shape, 0)
    pair = sums + pltpu.roll(sums, devices - 1, 0)
    logs = 0.5 * jnp.log(pair / count + 1e-06)
    log_norm[0, 0] = jnp.sum(jnp.where(row % 2 == 0, logs, 0.0)[:, :1]) / columns
    here = jnp.sum(jnp.where(row == 2 * lax.axis_index("col"), pair, 0.0), axis=0, keepdims=True)
    scale = lax.rsqrt(here / count + 1e-06)[:, : plan.chi]
    for d in range(n):
        for e in range(n):
            at = (d // 2) * plan.seg + (d % 2) * n + e
            new[d * n + e] = (image[pl.ds(at, half, stride=plan.xrows), :] * scale).astype(jnp.bfloat16)


def whole(memory, count):
    return [pl.BlockSpec(memory_space=memory) for _ in range(count)]


def absorb_row(mps, ket, left_proj, right_proj, bond_charge, new_charge, link_charge, vert_charge):
    half, chi, legs = left_proj.shape[1], left_proj.shape[2], left_proj.shape[3]
    phys = ket.shape[5]
    plan = Plan(chi, half, legs, phys)
    squared = legs * legs
    columns, sections = lax.axis_size("col"), lax.axis_size("sec")
    bf16, f32 = jnp.bfloat16, jnp.float32
    smem, vmem = pltpu.SMEM, pltpu.VMEM
    swap = [(i, 1 - i) for i in range(sections)]
    hbm = pltpu.HBM
    bond_next, fresh_next, link_next = from_behind((bond_charge, new_charge, link_charge), "col", -1)
    mine = jnp.transpose(mps[0], (1, 2, 0, 3)).reshape(squared, half, chi)
    other = lax.ppermute(mine, "sec", swap)
    pr_mine = from_behind(jnp.transpose(right_proj[0], (1, 2, 3, 0)).reshape(squared, half, chi), "col", -1)
    bond_next, fresh_next, link_next = lax.optimization_barrier((bond_next, fresh_next, link_next))
    left = jnp.transpose(left_proj[0], (2, 3, 0, 1)).reshape(squared, half, chi)
    flat_ket = jnp.transpose(ket[0], (0, 1, 2, 4, 3)).reshape(squared, squared * phys)
    fetched = [left, bond_charge, new_charge, link_charge, vert_charge] + plan.matrices() + plan.indices()
    in_smem = (3, 4)
    scratch = [(smem if i in in_smem else vmem)(x.shape, x.dtype) for i, x in enumerate(fetched)]
    scratch = [scratch[i] for i in (0, 1, 2, 3, 4)] + scratch[5:]
    lhs, *kets = pl.pallas_call(
        functools.partial(prep_kernel, plan),
        in_specs=whole(vmem, 1) + whole(hbm, len(fetched)),
        out_specs=whole(vmem, 6),
        out_shape=[
            jax.ShapeDtypeStruct((half * plan.lm, chi), bf16),
            jax.ShapeDtypeStruct((plan.rows2, plan.cols2), bf16),
            jax.ShapeDtypeStruct((plan.rows3, plan.cols3), bf16),
            jax.ShapeDtypeStruct((squared * phys, plan.cols2), jnp.int32),
            jax.ShapeDtypeStruct((plan.seg, plan.cols3), jnp.int32),
            jax.ShapeDtypeStruct((chi, 1), jnp.int32),
        ],
        scratch_shapes=[pltpu.VMEM((half * plan.lm, chi), f32)] + scratch + [pltpu.SemaphoreType.DMA((len(fetched),))],
        compiler_params=pltpu.CompilerParams(vmem_limit_bytes=12 << 20),
        cost_estimate=pl.CostEstimate(flops=FRONT_FLOPS // 8, bytes_accessed=1 << 20, transcendentals=0),
        name="prep",
    )(flat_ket, *[pltpu.with_memory_space_constraint(x, pltpu.HBM) for x in fetched])
    quads = half // QUAD
    ahead = quads // 3
    block = QUAD * plan.xrows
    lanes = plan.lanes
    step_scratch = [
        pltpu.VMEM((2, plan.pairs, plan.cols2, 2 * QUAD * lanes), bf16),
        pltpu.VMEM((2, plan.groups, plan.cols3, QUAD * lanes), bf16),
    ]
    operands = [link_next, bond_next, other, lhs] + kets
    operands += [pltpu.with_memory_space_constraint(x, pltpu.HBM) for x in (mine, vert_charge)]
    ms, k2, k3, w3_ahead = pl.pallas_call(
        functools.partial(front_kernel, plan, ahead),
        in_specs=whole(smem, 1) + whole(vmem, len(operands) - 3) + whole(hbm, 2),
        out_specs=whole(vmem, 4),
        out_shape=[
            jax.ShapeDtypeStruct((plan.pairs, plan.pairs, chi, 4 * lanes), bf16),
            jax.ShapeDtypeStruct((plan.rows2, plan.cols2), bf16),
            jax.ShapeDtypeStruct((plan.rows3, plan.cols3), bf16),
            jax.ShapeDtypeStruct((ahead, legs, block, legs * lanes), bf16),
        ],
        scratch_shapes=step_scratch
        + [
            pltpu.VMEM(mine.shape, bf16),
            pltpu.SMEM(vert_charge.shape, jnp.int32),
            pltpu.SemaphoreType.DMA((2,)),
        ],
        compiler_params=pltpu.CompilerParams(vmem_limit_bytes=VMEM_LIMIT),
        cost_estimate=pl.CostEstimate(flops=FRONT_FLOPS, bytes_accessed=1 << 20, transcendentals=0),
        name="front",
    )(*operands)
    pr_mine, w3_ahead = lax.optimization_barrier((pr_mine, w3_ahead))
    pr_other = lax.ppermute(pr_mine, "sec", swap)
    operands = [link_next, bond_next, fresh_next, lhs, ms, k2, k3, w3_ahead, pr_mine, pr_other]
    image, partial = pl.pallas_call(
        functools.partial(back_kernel, plan, ahead),
        in_specs=whole(smem, 1) + whole(vmem, len(operands) - 1),
        out_specs=whole(vmem, 2),
        out_shape=[
            jax.ShapeDtypeStruct((quads * block, chi), f32),
            jax.ShapeDtypeStruct((columns * sections, 1, LANES), f32),
        ],
        scratch_shapes=[pltpu.VMEM((legs, chi, legs * lanes), bf16)]
        + step_scratch
        + [pltpu.VMEM((2, legs, block, legs * lanes), bf16)],
        compiler_params=pltpu.CompilerParams(vmem_limit_bytes=VMEM_LIMIT),
        cost_estimate=pl.CostEstimate(flops=2 * FRONT_FLOPS, bytes_accessed=1 << 20, transcendentals=0),
        name="back",
    )(*operands)
    incoming = lax.all_to_all(partial, ("col", "sec"), 0, 0, tiled=True)
    new, log_norm = pl.pallas_call(
        functools.partial(finish_kernel, plan, float(chi * squared * chi), float(columns)),
        in_specs=whole(vmem, 2),
        out_specs=whole(vmem, 1) + whole(smem, 1),
        out_shape=[
            jax.ShapeDtypeStruct((squared, half, chi), bf16),
            jax.ShapeDtypeStruct((1, 1), f32),
        ],
        compiler_params=pltpu.CompilerParams(vmem_limit_bytes=8 << 20),
        name="finish",
    )(incoming.reshape(columns * sections, LANES), image)
    new_mps = jnp.transpose(new.reshape(legs, legs, half, chi), (2, 0, 1, 3))[None]
    return (new_mps, log_norm.reshape(()))


def solution(mesh):
    placed = (
        P("col", "sec", None, None, None),
        P("col", None, None, None, None, None),
        P("col", "sec", None, None, None),
        P("col", None, None, None, "sec"),
        P("col", None),
        P("col", None),
        P("col", None),
        P("col", None, None),
    )
    return jax.shard_map(
        absorb_row,
        mesh=mesh,
        in_specs=placed,
        out_specs=(P("col", "sec", None, None, None), P()),
        check_vma=False,
    )
```

time: 157 us -> 69.4 us (0.44)
  matrix products: 89.7 us -> 0 us
  Pallas kernels: 0 us -> 37.7 us
  blocking collectives: 48.6 us -> 13.4 us
  waiting for transfers between devices: 0.01 us -> 6.56 us
  other arithmetic: 4.45 us -> 0 us
  between operations: 3.22 us -> 0.84 us
    dot_general x4 -> x0, matrix products: 89.7 us -> none  [the longest x1 38.6 us: absorb(): jnp.einsum('xmvbdrp,vmesp->xbdres', second, masked_ket, preferred_element...]
    psum x2 -> x0, blocking collectives: 43.2 us -> none  [the longest x1 40.1 us: local(): total = lax.psum(jnp.sum(logs), 'col')]
    pallas_call x0 -> x4, Pallas kernels: none -> 37.7 us  [the longest x1 25 us: absorb_row(): pl.pallas_call(functools.partial(back_kernel, plan, ahead), in_specs=whol...]
    all_to_all x0 -> x1, blocking collectives: none -> 13.4 us  [absorb_row(): incoming = lax.all_to_all(partial, ('col', 'sec'), 0, 0, tiled=True)]
    all_gather x2 -> x0, blocking collectives: 5.46 us -> none  [the longest x1 2.82 us: local(): right_next = lax.all_gather(partial_next, 'sec', axis=4, tiled=True)]
    ppermute x4, waiting for transfers between devices: 0.01 us -> 4.77 us  [from_behind(): return lax.ppermute(x, axis, [(i, (i + by) % count) for i in range(count)])]
    ppermute x0 -> x2, waiting for transfers between devices: none -> 1.78 us  [the longest x1 1.78 us: absorb_row(): pr_other = lax.ppermute(pr_mine, 'sec', swap)]
    add x5 -> x0, other arithmetic: 1.61 us -> none  [the longest x1 0.74 us: absorb(): charge_here[None, :, None, None] + link_here[None, None, :, None]]
  transfers between devices with their start and end apart: 4 -> 6, of which waited for: 0 -> 2; matrix products, arithmetic and copies ran while one was open for 49% -> 2% of each run, Pallas kernels for 0% -> 17%
where the time goes in v3:
time: 69.4 us; the launch traced here: 69.2 us
  Pallas kernels  37.7 us (54%)
  blocking collectives  13.4 us (19%)
  starting transfers between devices  9.67 us (14%)
  waiting for transfers between devices  6.56 us (9%)
  local copies, waits for them, and re-layouts  1.04 us (1%)
  between operations  0.84 us (1%)
    pallas_call x1, Pallas kernels, absorb_row(): pl.pallas_call(functools.partial(back_kernel, plan, ahead), in_specs=whol...  25 us
    all_to_all x1, blocking collectives, absorb_row(): incoming = lax.all_to_all(partial, ('col', 'sec'), 0, 0, tiled=True)  13.4 us
    pallas_call x1, Pallas kernels, absorb_row(): pl.pallas_call(functools.partial(front_kernel, plan, ahead), in_specs=who...  9.5 us
    ppermute x4, starting transfers between devices, from_behind(): return lax.ppermute(x, axis, [(i, (i + by) % count) for i in range(count)])  9.04 us
    ppermute x4, waiting for transfers between devices, from_behind(): return lax.ppermute(x, axis, [(i, (i + by) % count) for i in range(count)])  4.77 us
    pallas_call x1, Pallas kernels, absorb_row(): pl.pallas_call(functools.partial(prep_kernel, plan), in_specs=whole(vmem,...  2.04 us
    ppermute x1, waiting for transfers between devices, absorb_row(): pr_other = lax.ppermute(pr_mine, 'sec', swap)  1.78 us
  transfers between devices with their start and end apart: 6, of which 2 were waited for; matrix products, arithmetic and copies ran while one was open for 2% of the time, Pallas kernels for 17%

profile of v3, /device:TPU:0, one launch (start us, length us, event | category | flops | bytes accessed | tf_op | source)
XLA Modules:
  0.0 69.2 jit_solution(5709947872672556672)
XLA Ops:
  0.6 0.6 collective-permute-start.3
  1.2 6.5 %collective-permute-start.4 = (bf16[36,48,96]{2,1,0:T(8,128)(2,1)}, bf16[36,48,96]{2,1,0:T(8,128)(2,1)S(1)}, u32[]{:S(2)}, u32[]{:S(2)}) collective-permute-start(bf16[36,48,96]{2,1,0:T(8,128)(2,1)} %bitcast.30), channel_id=1, source_target_pairs={{0,30},{2,0},{4,2},{6,4},{8,6},{10,8},{12,10},{14,12},{16,14},{18,... | collective-permute-start | bytes 995336 | tf_op jit(solution)/shard_map/ppermute | solution.py:23
  7.7 0.5 collective-permute-start
  8.3 1.4 %collective-permute-start.1 = (s32[1,96]{1,0:T(1,128)}, s32[1,96]{1,0:T(1,128)S(1)}, u32[]{:S(2)}, u32[]{:S(2)}) collective-permute-start(s32[1,96]{1,0:T(1,128)} %fresh_h.1), channel_id=1, source_target_pairs={{0,30},{2,0},{4,2},{6,4},{8,6},{10,8},{12,10},{14,12},{16,14},{18,... | collective-permute-start | bytes 1160 | tf_op jit(solution)/shard_map/ppermute | solution.py:23
  9.7 0.5 collective-permute-start.2
  10.2 1.0 %reshape.25.ket = bf16[36,72]{1,0:T(8,128)(2,1)S(1)} reshape(bf16[6,6,6,2,6]{4,3,2,1,0:T(2,128)(2,1)} %bitcast.27) | data formatting | bytes 10368 | tf_op jit(solution)/shard_map/reshape | solution.py:366
  11.3 2.0 %prep.1 = (bf16[1920,96]{1,0:T(8,128)(2,1)S(1)}, bf16[432,256]{1,0:T(8,128)(2,1)S(1)}, bf16[96,144]{1,0:T(8,128)(2,1)S(1)}, s32[72,256]{1,0:T(8,128)S(1)}, s32[16,144]{1,0:T(8,128)S(1)}, /*index=5*/s32[96,1]{1,0:T(8,128)S(1)}) custom-call(bf16[36,72]{1,0:T(8,128)(2,1)S(1)} %reshape.25.ket, bf16[36,48,96]{2,1,0:T(8,128)(2,1)} %bitcast.26, s32[1,96]{1,0:T(1,128)} %bond_h.1, ...), custom_call_target="tpu_custom_call" | custom-call | flops 134217728 | bytes 1048576 | tf_op jit(solution)/shard_map/prep/pallas_call | solution.py:371
  13.3 4.8 %collective-permute-done.2.link_next_s = s32[1,6]{1,0:T(1,128)S(1)} collective-permute-done((s32[1,6]{1,0:T(1,128)}, s32[1,6]{1,0:T(1,128)S(1)}, u32[]{:S(2)}, u32[]{:S(2)}) %collective-permute-start.2) | collective-permute-done | bytes 56 | tf_op jit(solution)/shard_map/ppermute | solution.py:23
  18.1 0.0 collective-permute-done.bond_next_v
  18.1 0.0 collective-permute-done.1.fresh_next_v
  18.1 0.0 collective-permute-done.3.other
  18.1 9.5 %front.1 = (bf16[3,3,96,512]{3,2,1,0:T(8,128)(2,1)S(1)}, bf16[432,256]{1,0:T(8,128)(2,1)S(1)}, bf16[96,144]{1,0:T(8,128)(2,1)S(1)}, bf16[4,6,192,768]{3,2,1,0:T(8,128)(2,1)S(1)}) custom-call(s32[1,6]{1,0:T(1,128)S(1)} %collective-permute-done.2.link_next_s, s32[1,96]{1,0:T(1,128)S(1)} %collective-permute-done.bond_next_v, ...), custom_call_target="tpu_custom_call" | custom-call | flops 1073741824 | bytes 1048576 | tf_op jit(solution)/shard_map/front/pallas_call | solution.py:398
  27.6 0.0 collective-permute-done.4.pr_mine
  27.6 0.1 collective-permute-start.5
  27.7 1.8 %collective-permute-done.5.pr_other = bf16[36,48,96]{2,1,0:T(8,128)(2,1)S(1)} collective-permute-done((bf16[36,48,96]{2,1,0:T(8,128)(2,1)S(1)}, bf16[36,48,96]{2,1,0:T(8,128)(2,1)S(1)}, u32[]{:S(2)}, u32[]{:S(2)}) %collective-permute-start.5) | collective-permute-done | bytes 331808 | tf_op jit(solution)/shard_map/ppermute | solution.py:419
  29.5 25.0 %back.1 = (f32[2304,96]{1,0:T(8,128)S(1)}, f32[32,1,128]{2,1,0:T(1,128)S(1)}) custom-call(s32[1,6]{1,0:T(1,128)S(1)} %collective-permute-done.2.link_next_s, s32[1,96]{1,0:T(1,128)S(1)} %collective-permute-done.bond_next_v, s32[1,96]{1,0:T(1,128)S(1)} %collective-permute-done.1.fresh_next_v, bf16[1920,96]{1,0:T(8,128)(2,1)S(1)} %get-tuple-element.24.lhs, ...), custom_call_target="tpu_custom_call" | custom-call | flops 2147483648 | bytes 1048576 | tf_op jit(solution)/shard_map/back/pallas_call | solution.py:421
  54.5 13.4 %all_to_all.5 = f32[32,1,128]{2,1,0:T(1,128)S(1)} all-to-all(f32[32,1,128]{2,1,0:T(1,128)S(1)} %get-tuple-element.36), channel_id=1, replica_groups=mesh['col'=16,'sec'=2] {'col','sec'}, dimensions={0} | all-to-all | bytes 32768 | tf_op jit(solution)/shard_map/all_to_all | solution.py:436
  68.0 1.1 %finish.1 = (bf16[36,48,96]{2,1,0:T(8,128)(2,1)}, f32[1,1]{1,0:T(1,128)}) custom-call(f32[32,128]{1,0:T(8,128)S(1)} %bitcast.25, f32[2304,96]{1,0:T(8,128)S(1)} %get-tuple-element.37.image), custom_call_target="tpu_custom_call" | custom-call | tf_op jit(solution)/shard_map/finish/pallas_call | solution.py:437
Async XLA Ops:
  0.6 17.5 %collective-permute-start.3 = (bf16[36,48,96]{2,1,0:T(8,128)(2,1)}, bf16[36,48,96]{2,1,0:T(8,128)(2,1)S(1)}, u32[]{:S(2)}, u32[]{:S(2)}) collective-permute-start(bf16[36,48,96]{2,1,0:T(8,128)(2,1)} %bitcast.28), channel_id=1, source_target_pairs={{0,1},{1,0},{2,3},{3,2},{4,5},{5,4},{6,7},{7,6},{8,9},{9,8},{10,11... | collective-permute-start | bytes 995336 | tf_op jit(solution)/shard_map/ppermute | solution.py:362
  1.2 26.4 %collective-permute-start.4 = (bf16[36,48,96]{2,1,0:T(8,128)(2,1)}, bf16[36,48,96]{2,1,0:T(8,128)(2,1)S(1)}, u32[]{:S(2)}, u32[]{:S(2)}) collective-permute-start(bf16[36,48,96]{2,1,0:T(8,128)(2,1)} %bitcast.30), channel_id=1, source_target_pairs={{0,30},{2,0},{4,2},{6,4},{8,6},{10,8},{12,10},{14,12},{16,14},{18,... | collective-permute-start | bytes 995336 | tf_op jit(solution)/shard_map/ppermute | solution.py:23
  7.7 10.4 %collective-permute-start = (s32[1,96]{1,0:T(1,128)}, s32[1,96]{1,0:T(1,128)S(1)}, u32[]{:S(2)}, u32[]{:S(2)}) collective-permute-start(s32[1,96]{1,0:T(1,128)} %bond_h.1), channel_id=1, source_target_pairs={{0,30},{2,0},{4,2},{6,4},{8,6},{10,8},{12,10},{14,12},{16,14},{18,... | collective-permute-start | bytes 1160 | tf_op jit(solution)/shard_map/ppermute | solution.py:23
  8.3 9.8 %collective-permute-start.1 = (s32[1,96]{1,0:T(1,128)}, s32[1,96]{1,0:T(1,128)S(1)}, u32[]{:S(2)}, u32[]{:S(2)}) collective-permute-start(s32[1,96]{1,0:T(1,128)} %fresh_h.1), channel_id=1, source_target_pairs={{0,30},{2,0},{4,2},{6,4},{8,6},{10,8},{12,10},{14,12},{16,14},{18,... | collective-permute-start | bytes 1160 | tf_op jit(solution)/shard_map/ppermute | solution.py:23
  9.7 8.4 %collective-permute-start.2 = (s32[1,6]{1,0:T(1,128)}, s32[1,6]{1,0:T(1,128)S(1)}, u32[]{:S(2)}, u32[]{:S(2)}) collective-permute-start(s32[1,6]{1,0:T(1,128)} %link_h.1), channel_id=1, source_target_pairs={{0,30},{2,0},{4,2},{6,4},{8,6},{10,8},{12,10},{14,12},{16,14},{18,... | collective-permute-start | bytes 80 | tf_op jit(solution)/shard_map/ppermute | solution.py:23
  27.6 1.9 %collective-permute-start.5 = (bf16[36,48,96]{2,1,0:T(8,128)(2,1)S(1)}, bf16[36,48,96]{2,1,0:T(8,128)(2,1)S(1)}, u32[]{:S(2)}, u32[]{:S(2)}) collective-permute-start(bf16[36,48,96]{2,1,0:T(8,128)(2,1)S(1)} %collective-permute-done.4.pr_mine), channel_id=1, source_target_pairs={{0,1},{1,0},{2,3},{3,2},{4,5},{5,4},{6,7},{7,6},{8,9},{9,8},{10,11... | collective-permute-start | bytes 995336 | tf_op jit(solution)/shard_map/ppermute | solution.py:419

commit v4 on v3

--- a/solution.py
+++ b/solution.py
@@ -176,34 +176,72 @@
     return ((first, sec), (second, 1 - sec))
 
 
-def first_two(plan, left, ms, k2, w1, w2, vp):
-    lanes, lm, gr = plan.lanes, plan.lm, plan.group_rows
-    bf16 = jnp.bfloat16
+def pack_lanes(parts, chi):
+    lane = lax.broadcasted_iota(jnp.int32, parts[0].shape, 1)
+    tiles = []
+    for x, part in enumerate(parts):
+        first, shift = divmod(x * chi, LANES)
+        rolled = pltpu.roll(part, shift, 1) if shift else part
+        if first == len(tiles):
+            tiles.append(rolled)
+        else:
+            tiles[first] = jnp.where(lane < shift, tiles[first], rolled)
+        if shift + chi > LANES:
+            tiles.append(rolled)
+    return tiles
+
+
+def unpack_lanes(tiles, chi, count):
+    lane = lax.broadcasted_iota(jnp.int32, tiles[0].shape, 1)
+    parts = []
+    for x in range(count):
+        first, shift = divmod(x * chi, LANES)
+        part = tiles[first]
+        if shift + chi > LANES:
+            part = jnp.where(lane >= shift, part, tiles[first + 1])
+        parts.append(pltpu.roll(part, LANES - shift, 1) if shift else part)
+    return parts
+
+
+def first(plan, left, ms, w1, vp):
+    chi, lm = plan.chi, plan.lm
     for up in range(plan.pairs):
         both = dot(left, ms[up, vp])
-        for x in range(QUAD):
-            part = both[x * lm : (x + 1) * lm]
-            stacked = jnp.concatenate([part[:, : 2 * lanes], part[:, 2 * lanes :]], axis=0)
-            w1[vp, up * 2 * lm : (up + 1) * 2 * lm, x * 2 * lanes : (x + 1) * 2 * lanes] = stacked.astype(bf16)
-    for h in range(QUAD // 2):
-        out = dot(k2[...], w1[vp, :, h * 4 * lanes : (h + 1) * 4 * lanes])
-        for g in range(plan.groups):
-            part = out[g * gr : (g + 1) * gr]
-            for j in range(2):
-                x = 2 * h + j
-                low, high = part[:, 2 * j * lanes : (2 * j + 1) * lanes], part[:, (2 * j + 1) * lanes : (2 * j + 2) * lanes]
-                stacked = jnp.concatenate([low, high], axis=0)
-                w2[g, vp * 2 * gr : (vp + 1) * 2 * gr, x * lanes : (x + 1) * lanes] = stacked.astype(bf16)
+        for k in range(2):
+            parts = []
+            for x in range(QUAD):
+                rows = both[x * lm : (x + 1) * lm]
+                parts.append(
+                    jnp.concatenate([rows[:, c * LANES : (c + 1) * LANES] for c in (2 * k, 2 * k + 1)], axis=0)
+                )
+            for t, tile in enumerate(pack_lanes(parts, chi)):
+                at = (2 * t + k) * LANES
+                w1[vp, up * 2 * lm : (up + 1) * 2 * lm, at : at + LANES] = tile.astype(jnp.bfloat16)
+
+
+def second(plan, k2, w1, w2, vp, half_of_oct):
+    gr, wide = plan.group_rows, QUAD * plan.chi
+    out = dot(k2[...], w1[vp])
+    for g in range(plan.groups):
+        part = out[g * gr : (g + 1) * gr]
+        for t in range(wide // LANES):
+            pair = [part[:, c * LANES : (c + 1) * LANES] for c in (2 * t, 2 * t + 1)]
+            at = half_of_oct * wide + t * LANES
+            w2[g, vp * 2 * gr : (vp + 1) * 2 * gr, at : at + LANES] = jnp.concatenate(pair, axis=0).astype(jnp.bfloat16)
 
 
 def third(plan, k3, w2, w3, g):
-    lanes, seg = plan.lanes, plan.seg
+    seg = plan.seg
     r, dp = g // plan.pairs, g % plan.pairs
-    out = dot(k3[...], w2[g]).astype(jnp.bfloat16)
-    for s in range(plan.legs):
-        for x in range(QUAD):
-            at = x * plan.xrows + dp * seg
-            w3[r, at : at + seg, s * lanes : (s + 1) * lanes] = out[s * seg : (s + 1) * seg, x * lanes : (x + 1) * lanes]
+    out = dot(k3[...], w2[g])
+    per = QUAD * plan.chi // LANES
+    for h in range(2):
+        tiles = [out[:, t * LANES : (t + 1) * LANES] for t in range(h * per, (h + 1) * per)]
+        for x, part in enumerate(unpack_lanes(tiles, plan.chi, QUAD)):
+            part = part.astype(jnp.bfloat16)
+            at = (h * QUAD + x) * plan.xrows + dp * seg
+            for s in range(plan.legs):
+                w3[r, at : at + seg, s * LANES : (s + 1) * LANES] = part[s * seg : (s + 1) * seg]
 
 
 def fourth(w3, pr, r):
@@ -220,10 +258,10 @@
 
 
 def front_kernel(
-    plan, ahead,
+    plan,
     link_next_s, bond_next_v, other, lhs, k2_all, k3_all, gap2, gap3, bond_col, mine_h, vert_h,
-    ms, k2, k3, w3,
-    w1, w2, mine, vert_s, sems,
+    ms, k2, k3, w2, w3,
+    w1, w2_first, mine, vert_s, sems,
 ):
     n, chi, half, lanes = plan.legs, plan.chi, plan.half, plan.lanes
     bf16 = jnp.bfloat16
@@ -249,26 +287,33 @@
             for v in range(n):
                 keep = gap == upper[u] - upper[v]
                 val = jnp.where(keep, src[u * n + v].astype(jnp.float32), 0.0)
-                lane = (u % 2 * 2 + v % 2) * lanes
+                lane = (v % 2 * 2 + u % 2) * lanes
                 ms[u // 2, v // 2, pl.ds(at, half), lane : lane + chi] = val.astype(bf16)
     pad = n * plan.lm
     w1[:, :, pad:, :] = jnp.zeros((2, plan.pairs, plan.cols2 - pad, w1.shape[3]), bf16)
-    per_g = plan.groups // plan.pairs
-    for q in range(ahead + 1):
-        for vp in range(plan.pairs):
-            if q < ahead:
-                first_two(plan, quad_rows(lhs, plan, q), ms, k2, w1.at[q % 2], w2.at[q % 2], vp)
-            if q > 0:
-                for g in range(vp * per_g, (vp + 1) * per_g):
-                    third(plan, k3, w2.at[(q - 1) % 2], w3.at[q - 1], g)
+    phases = [(o, vp, h) for o in range(2) for vp in range(plan.pairs) for h in range(2)]
+    per_g = plan.groups // (2 * plan.pairs)
+
+    def lead(o, vp, h):
+        first(plan, quad_rows(lhs, plan, 2 * o + h), ms, w1.at[h], vp)
+
+    lead(*phases[0])
+    for i, (o, vp, h) in enumerate(phases):
+        if i + 1 < len(phases):
+            lead(*phases[i + 1])
+        if o:
+            at = (2 * vp + h) * per_g
+            for g in range(at, at + per_g):
+                third(plan, k3, w2_first, w3, g)
+        second(plan, k2, w1.at[h], w2 if o else w2_first, vp, h)
 
 
 def back_kernel(
-    plan, ahead,
+    plan,
     link_next_s,
-    bond_next_v, fresh_next_v, lhs, ms, k2, k3, w3_ahead, pr_mine, pr_other,
-    image, partial,
-    pr, w1, w2, w3,
+    bond_next_v, fresh_next_v, lhs, ms, k2, k3, w2_in, w3_in, pr_mine, pr_other,
+    image, partial, w2_odd, w3_even,
+    pr, w1, w2_even, w3_odd,
 ):
     n, chi, half, lanes = plan.legs, plan.chi, plan.half, plan.lanes
     bf16 = jnp.bfloat16
@@ -286,44 +331,50 @@
     pad = n * plan.lm
     w1[:, :, pad:, :] = jnp.zeros((2, plan.pairs, plan.cols2 - pad, w1.shape[3]), bf16)
 
-    block = QUAD * plan.xrows
-    per_g = plan.groups // plan.pairs
-    per_r = n // plan.pairs
-
-    def put(quad, total):
-        image[pl.ds(pl.multiple_of(quad * block, 8), block), :] = total
+    del w2_in, w3_in
+    block = 2 * QUAD * plan.xrows
+    per_g = plan.groups // (2 * plan.pairs)
+    per_r = n // (2 * plan.pairs)
+    w2, w3 = (w2_even, w2_odd), (w3_even, w3_odd)
+
+    def put(oct, total):
+        image[pl.ds(pl.multiple_of(oct * block, 8), block), :] = total
         return jnp.sum(total * total)
 
-    def body(step, square_sum):
-        early = None
-        for k in range(2):
-            total = None
-            for vp in range(plan.pairs):
-                left = quad_rows(lhs, plan, ahead + 2 * step + k)
-                first_two(plan, left, ms, k2, w1.at[k], w2.at[k], vp)
-                for g in range(vp * per_g, (vp + 1) * per_g):
-                    third(plan, k3, w2.at[1 - k], w3.at[1 - k], g)
-                for r in range(vp * per_r, (vp + 1) * per_r):
-                    total = add(total, fourth(w3.at[k], pr, r))
-                    if r % 2 == k:
-                        early = add(early, fourth(w3_ahead.at[step], pr, r))
-            square_sum = square_sum + jnp.where(step > 0, put(ahead - 2 + 2 * step + k, total), 0.0)
-        return square_sum + put(step, early)
-
-    quads = half // QUAD
-    steps = (quads - ahead) // 2
-    square_sum = lax.fori_loop(0, steps, body, jnp.float32(0.0))
+    def body(j, square_sum):
+        def lead(k, vp, h):
+            first(plan, quad_rows(lhs, plan, 2 * (2 * j + k + 2) + h), ms, w1.at[h], vp)
+
+        phases = [(k, vp, h) for k in range(2) for vp in range(plan.pairs) for h in range(2)]
+        total = None
+        lead(*phases[0])
+        for i, (k, vp, h) in enumerate(phases):
+            if i + 1 < len(phases):
+                lead(*phases[i + 1])
+            phase = 2 * vp + h
+            for g in range(phase * per_g, (phase + 1) * per_g):
+                third(plan, k3, w2[1 - k], w3[1 - k], g)
+            for r in range(phase * per_r, (phase + 1) * per_r):
+                total = add(total, fourth(w3[k], pr, r))
+            second(plan, k2, w1.at[h], w2[k], vp, h)
+            if phase == 2 * plan.pairs - 1:
+                square_sum = square_sum + put(2 * j + k, total)
+                total = None
+        return square_sum
+
+    octs = half // (2 * QUAD)
+    square_sum = lax.fori_loop(0, (octs - 2) // 2, body, jnp.float32(0.0))
     total = None
     for g in range(plan.groups):
-        third(plan, k3, w2.at[1], w3.at[1], g)
+        third(plan, k3, w2_odd, w3_odd, g)
         if g % plan.pairs == 0:
-            total = add(total, fourth(w3.at[0], pr, g // plan.pairs))
-    square_sum = square_sum + put(quads - 2, total)
+            total = add(total, fourth(w3_even, pr, g // plan.pairs))
+    square_sum = square_sum + put(octs - 2, total)
     even = odd = None
     for r in range(0, n, 2):
-        even = add(even, fourth(w3.at[1], pr, r))
-        odd = add(odd, fourth(w3.at[1], pr, r + 1))
-    square_sum = square_sum + put(quads - 1, even + odd)
+        even = add(even, fourth(w3_odd, pr, r))
+        odd = add(odd, fourth(w3_odd, pr, r + 1))
+    square_sum = square_sum + put(octs - 1, even + odd)
     partial[...] = jnp.full_like(partial, square_sum)
 
 
@@ -385,28 +436,31 @@
         cost_estimate=pl.CostEstimate(flops=FRONT_FLOPS // 8, bytes_accessed=1 << 20, transcendentals=0),
         name="prep",
     )(flat_ket, *[pltpu.with_memory_space_constraint(x, pltpu.HBM) for x in fetched])
-    quads = half // QUAD
-    ahead = quads // 3
-    block = QUAD * plan.xrows
+    octs = half // (2 * QUAD)
+    if half % (2 * QUAD) or octs % 2 or (QUAD * chi) % LANES:
+        raise ValueError("half")
+    block = 2 * QUAD * plan.xrows
     lanes = plan.lanes
-    step_scratch = [
-        pltpu.VMEM((2, plan.pairs, plan.cols2, 2 * QUAD * lanes), bf16),
-        pltpu.VMEM((2, plan.groups, plan.cols3, QUAD * lanes), bf16),
-    ]
+    wide = 2 * QUAD * chi
+    w1_shape = (2, plan.pairs, plan.cols2, wide)
+    w2_shape = jax.ShapeDtypeStruct((plan.groups, plan.cols3, wide), bf16)
+    w3_shape = jax.ShapeDtypeStruct((legs, block, legs * lanes), bf16)
     operands = [link_next, bond_next, other, lhs] + kets
     operands += [pltpu.with_memory_space_constraint(x, pltpu.HBM) for x in (mine, vert_charge)]
-    ms, k2, k3, w3_ahead = pl.pallas_call(
-        functools.partial(front_kernel, plan, ahead),
+    ms, k2, k3, w2, w3 = pl.pallas_call(
+        functools.partial(front_kernel, plan),
         in_specs=whole(smem, 1) + whole(vmem, len(operands) - 3) + whole(hbm, 2),
-        out_specs=whole(vmem, 4),
+        out_specs=whole(vmem, 5),
         out_shape=[
             jax.ShapeDtypeStruct((plan.pairs, plan.pairs, chi, 4 * lanes), bf16),
             jax.ShapeDtypeStruct((plan.rows2, plan.cols2), bf16),
             jax.ShapeDtypeStruct((plan.rows3, plan.cols3), bf16),
-            jax.ShapeDtypeStruct((ahead, legs, block, legs * lanes), bf16),
+            w2_shape,
+            w3_shape,
         ],
-        scratch_shapes=step_scratch
-        + [
+        scratch_shapes=[
+            pltpu.VMEM(w1_shape, bf16),
+            pltpu.VMEM(w2_shape.shape, bf16),
             pltpu.VMEM(mine.shape, bf16),
             pltpu.SMEM(vert_charge.shape, jnp.int32),
             pltpu.SemaphoreType.DMA((2,)),
@@ -415,20 +469,26 @@
         cost_estimate=pl.CostEstimate(flops=FRONT_FLOPS, bytes_accessed=1 << 20, transcendentals=0),
         name="front",
     )(*operands)
-    pr_mine, w3_ahead = lax.optimization_barrier((pr_mine, w3_ahead))
+    pr_mine, w3 = lax.optimization_barrier((pr_mine, w3))
     pr_other = lax.ppermute(pr_mine, "sec", swap)
-    operands = [link_next, bond_next, fresh_next, lhs, ms, k2, k3, w3_ahead, pr_mine, pr_other]
-    image, partial = pl.pallas_call(
-        functools.partial(back_kernel, plan, ahead),
+    operands = [link_next, bond_next, fresh_next, lhs, ms, k2, k3, w2, w3, pr_mine, pr_other]
+    image, partial, _, _ = pl.pallas_call(
+        functools.partial(back_kernel, plan),
         in_specs=whole(smem, 1) + whole(vmem, len(operands) - 1),
-        out_specs=whole(vmem, 2),
+        out_specs=whole(vmem, 4),
         out_shape=[
-            jax.ShapeDtypeStruct((quads * block, chi), f32),
+            jax.ShapeDtypeStruct((octs * block, chi), f32),
             jax.ShapeDtypeStruct((columns * sections, 1, LANES), f32),
+            w2_shape,
+            w3_shape,
         ],
-        scratch_shapes=[pltpu.VMEM((legs, chi, legs * lanes), bf16)]
-        + step_scratch
-        + [pltpu.VMEM((2, legs, block, legs * lanes), bf16)],
+        input_output_aliases={7: 2, 8: 3},
+        scratch_shapes=[
+            pltpu.VMEM((legs, chi, legs * lanes), bf16),
+            pltpu.VMEM(w1_shape, bf16),
+            pltpu.VMEM(w2_shape.shape, bf16),
+            pltpu.VMEM(w3_shape.shape, bf16),
+        ],
         compiler_params=pltpu.CompilerParams(vmem_limit_bytes=VMEM_LIMIT),
         cost_estimate=pl.CostEstimate(flops=2 * FRONT_FLOPS, bytes_accessed=1 << 20, transcendentals=0),
         name="back",

time: 69.4 us -> 61 us (0.88)
  Pallas kernels: 37.7 us -> 29.3 us
    pallas_call x2, Pallas kernels: 34.5 us -> 26.2 us  [the longest x1 19.4 us: absorb_row(): pl.pallas_call(functools.partial(back_kernel, plan), in_specs=whole(smem,...]
  transfers between devices with their start and end apart: 6 -> 6, of which waited for: 2 -> 2; matrix products, arithmetic and copies ran while one was open for 2% -> 2% of each run, Pallas kernels for 17% -> 14%
where the time goes in v4:
time: 61 us; the launch traced here: 60.8 us
  Pallas kernels  29.3 us (48%)
  blocking collectives  13.4 us (22%)
  starting transfers between devices  9.67 us (16%)
  waiting for transfers between devices  6.56 us (11%)
  local copies, waits for them, and re-layouts  1.04 us (2%)
  between operations  0.84 us (1%)
    pallas_call x1, Pallas kernels, absorb_row(): pl.pallas_call(functools.partial(back_kernel, plan), in_specs=whole(smem,...  19.4 us
    all_to_all x1, blocking collectives, absorb_row(): incoming = lax.all_to_all(partial, ('col', 'sec'), 0, 0, tiled=True)  13.4 us
    ppermute x4, starting transfers between devices, from_behind(): return lax.ppermute(x, axis, [(i, (i + by) % count) for i in range(count)])  9.04 us
    pallas_call x1, Pallas kernels, absorb_row(): pl.pallas_call(functools.partial(front_kernel, plan), in_specs=whole(smem...  6.74 us
    ppermute x4, waiting for transfers between devices, from_behind(): return lax.ppermute(x, axis, [(i, (i + by) % count) for i in range(count)])  4.77 us
    pallas_call x1, Pallas kernels, absorb_row(): pl.pallas_call(functools.partial(prep_kernel, plan), in_specs=whole(vmem,...  2.04 us
    ppermute x1, waiting for transfers between devices, absorb_row(): pr_other = lax.ppermute(pr_mine, 'sec', swap)  1.78 us
  transfers between devices with their start and end apart: 6, of which 2 were waited for; matrix products, arithmetic and copies ran while one was open for 2% of the time, Pallas kernels for 14%

profile of v4, /device:TPU:0, one launch (start us, length us, event | category | flops | bytes accessed | tf_op | source)
XLA Modules:
  0.0 60.8 jit_solution(15435384320197423605)
XLA Ops:
  0.6 0.6 collective-permute-start.3
  1.2 6.5 %collective-permute-start.4 = (bf16[36,48,96]{2,1,0:T(8,128)(2,1)}, bf16[36,48,96]{2,1,0:T(8,128)(2,1)S(1)}, u32[]{:S(2)}, u32[]{:S(2)}) collective-permute-start(bf16[36,48,96]{2,1,0:T(8,128)(2,1)} %bitcast.30), channel_id=1, source_target_pairs={{0,30},{2,0},{4,2},{6,4},{8,6},{10,8},{12,10},{14,12},{16,14},{18,... | collective-permute-start | bytes 995336 | tf_op jit(solution)/shard_map/ppermute | solution.py:23
  7.7 0.5 collective-permute-start
  8.3 1.4 %collective-permute-start.1 = (s32[1,96]{1,0:T(1,128)}, s32[1,96]{1,0:T(1,128)S(1)}, u32[]{:S(2)}, u32[]{:S(2)}) collective-permute-start(s32[1,96]{1,0:T(1,128)} %fresh_h.1), channel_id=1, source_target_pairs={{0,30},{2,0},{4,2},{6,4},{8,6},{10,8},{12,10},{14,12},{16,14},{18,... | collective-permute-start | bytes 1160 | tf_op jit(solution)/shard_map/ppermute | solution.py:23
  9.7 0.5 collective-permute-start.2
  10.2 1.0 %reshape.25.ket = bf16[36,72]{1,0:T(8,128)(2,1)S(1)} reshape(bf16[6,6,6,2,6]{4,3,2,1,0:T(2,128)(2,1)} %bitcast.27) | data formatting | bytes 10368 | tf_op jit(solution)/shard_map/reshape | solution.py:417
  11.3 2.0 %prep.1 = (bf16[1920,96]{1,0:T(8,128)(2,1)S(1)}, bf16[432,256]{1,0:T(8,128)(2,1)S(1)}, bf16[96,144]{1,0:T(8,128)(2,1)S(1)}, s32[72,256]{1,0:T(8,128)S(1)}, s32[16,144]{1,0:T(8,128)S(1)}, /*index=5*/s32[96,1]{1,0:T(8,128)S(1)}) custom-call(bf16[36,72]{1,0:T(8,128)(2,1)S(1)} %reshape.25.ket, bf16[36,48,96]{2,1,0:T(8,128)(2,1)} %bitcast.26, s32[1,96]{1,0:T(1,128)} %bond_h.1, ...), custom_call_target="tpu_custom_call" | custom-call | flops 134217728 | bytes 1048576 | tf_op jit(solution)/shard_map/prep/pallas_call | solution.py:422
  13.3 4.8 %collective-permute-done.2.link_next_s = s32[1,6]{1,0:T(1,128)S(1)} collective-permute-done((s32[1,6]{1,0:T(1,128)}, s32[1,6]{1,0:T(1,128)S(1)}, u32[]{:S(2)}, u32[]{:S(2)}) %collective-permute-start.2) | collective-permute-done | bytes 56 | tf_op jit(solution)/shard_map/ppermute | solution.py:23
  18.1 0.0 collective-permute-done.bond_next_v
  18.1 0.0 collective-permute-done.1.fresh_next_v
  18.1 0.0 collective-permute-done.3.other
  18.1 6.7 %front.1 = (bf16[3,3,96,512]{3,2,1,0:T(8,128)(2,1)S(1)}, bf16[432,256]{1,0:T(8,128)(2,1)S(1)}, bf16[96,144]{1,0:T(8,128)(2,1)S(1)}, bf16[18,144,768]{2,1,0:T(8,128)(2,1)S(1)}, bf16[6,384,768]{2,1,0:T(8,128)(2,1)S(1)}) custom-call(s32[1,6]{1,0:T(1,128)S(1)} %collective-permute-done.2.link_next_s, s32[1,96]{1,0:T(1,128)S(1)} %collective-permute-done.bond_next_v, ...), custom_call_target="tpu_custom_call" | custom-call | flops 1073741824 | bytes 1048576 | tf_op jit(solution)/shard_map/front/pallas_call | solution.py:450
  24.8 0.0 collective-permute-done.4.pr_mine
  24.9 0.1 collective-permute-start.5
  24.9 1.8 %collective-permute-done.5.pr_other = bf16[36,48,96]{2,1,0:T(8,128)(2,1)S(1)} collective-permute-done((bf16[36,48,96]{2,1,0:T(8,128)(2,1)S(1)}, bf16[36,48,96]{2,1,0:T(8,128)(2,1)S(1)}, u32[]{:S(2)}, u32[]{:S(2)}) %collective-permute-start.5) | collective-permute-done | bytes 331808 | tf_op jit(solution)/shard_map/ppermute | solution.py:473
  26.7 19.4 %back.1 = (f32[2304,96]{1,0:T(8,128)S(1)}, f32[32,1,128]{2,1,0:T(1,128)S(1)}, bf16[18,144,768]{2,1,0:T(8,128)(2,1)S(1)}, bf16[6,384,768]{2,1,0:T(8,128)(2,1)S(1)}) custom-call(s32[1,6]{1,0:T(1,128)S(1)} %collective-permute-done.2.link_next_s, s32[1,96]{1,0:T(1,128)S(1)} %collective-permute-done.bond_next_v, ...), custom_call_target="tpu_custom_call", output_to_operand_aliasing={{2}: (7, {}), {3}: (8, {})} | custom-call | flops 2147483648 | bytes 1048576 | tf_op jit(solution)/shard_map/back/pallas_call | solution.py:475
  46.1 13.4 %all_to_all.5 = f32[32,1,128]{2,1,0:T(1,128)S(1)} all-to-all(f32[32,1,128]{2,1,0:T(1,128)S(1)} %get-tuple-element.38), channel_id=1, replica_groups=mesh['col'=16,'sec'=2] {'col','sec'}, dimensions={0} | all-to-all | bytes 32768 | tf_op jit(solution)/shard_map/all_to_all | solution.py:496
  59.6 1.1 %finish.1 = (bf16[36,48,96]{2,1,0:T(8,128)(2,1)}, f32[1,1]{1,0:T(1,128)}) custom-call(f32[32,128]{1,0:T(8,128)S(1)} %bitcast.25, f32[2304,96]{1,0:T(8,128)S(1)} %get-tuple-element.39.image), custom_call_target="tpu_custom_call" | custom-call | tf_op jit(solution)/shard_map/finish/pallas_call | solution.py:497
Async XLA Ops:
  0.6 17.5 %collective-permute-start.3 = (bf16[36,48,96]{2,1,0:T(8,128)(2,1)}, bf16[36,48,96]{2,1,0:T(8,128)(2,1)S(1)}, u32[]{:S(2)}, u32[]{:S(2)}) collective-permute-start(bf16[36,48,96]{2,1,0:T(8,128)(2,1)} %bitcast.28), channel_id=1, source_target_pairs={{0,1},{1,0},{2,3},{3,2},{4,5},{5,4},{6,7},{7,6},{8,9},{9,8},{10,11... | collective-permute-start | bytes 995336 | tf_op jit(solution)/shard_map/ppermute | solution.py:413
  1.2 23.7 %collective-permute-start.4 = (bf16[36,48,96]{2,1,0:T(8,128)(2,1)}, bf16[36,48,96]{2,1,0:T(8,128)(2,1)S(1)}, u32[]{:S(2)}, u32[]{:S(2)}) collective-permute-start(bf16[36,48,96]{2,1,0:T(8,128)(2,1)} %bitcast.30), channel_id=1, source_target_pairs={{0,30},{2,0},{4,2},{6,4},{8,6},{10,8},{12,10},{14,12},{16,14},{18,... | collective-permute-start | bytes 995336 | tf_op jit(solution)/shard_map/ppermute | solution.py:23
  7.7 10.4 %collective-permute-start = (s32[1,96]{1,0:T(1,128)}, s32[1,96]{1,0:T(1,128)S(1)}, u32[]{:S(2)}, u32[]{:S(2)}) collective-permute-start(s32[1,96]{1,0:T(1,128)} %bond_h.1), channel_id=1, source_target_pairs={{0,30},{2,0},{4,2},{6,4},{8,6},{10,8},{12,10},{14,12},{16,14},{18,... | collective-permute-start | bytes 1160 | tf_op jit(solution)/shard_map/ppermute | solution.py:23
  8.3 9.8 %collective-permute-start.1 = (s32[1,96]{1,0:T(1,128)}, s32[1,96]{1,0:T(1,128)S(1)}, u32[]{:S(2)}, u32[]{:S(2)}) collective-permute-start(s32[1,96]{1,0:T(1,128)} %fresh_h.1), channel_id=1, source_target_pairs={{0,30},{2,0},{4,2},{6,4},{8,6},{10,8},{12,10},{14,12},{16,14},{18,... | collective-permute-start | bytes 1160 | tf_op jit(solution)/shard_map/ppermute | solution.py:23
  9.7 8.4 %collective-permute-start.2 = (s32[1,6]{1,0:T(1,128)}, s32[1,6]{1,0:T(1,128)S(1)}, u32[]{:S(2)}, u32[]{:S(2)}) collective-permute-start(s32[1,6]{1,0:T(1,128)} %link_h.1), channel_id=1, source_target_pairs={{0,30},{2,0},{4,2},{6,4},{8,6},{10,8},{12,10},{14,12},{16,14},{18,... | collective-permute-start | bytes 80 | tf_op jit(solution)/shard_map/ppermute | solution.py:23
  24.9 1.9 %collective-permute-start.5 = (bf16[36,48,96]{2,1,0:T(8,128)(2,1)S(1)}, bf16[36,48,96]{2,1,0:T(8,128)(2,1)S(1)}, u32[]{:S(2)}, u32[]{:S(2)}) collective-permute-start(bf16[36,48,96]{2,1,0:T(8,128)(2,1)S(1)} %collective-permute-done.4.pr_mine), channel_id=1, source_target_pairs={{0,1},{1,0},{2,3},{3,2},{4,5},{5,4},{6,7},{7,6},{8,9},{9,8},{10,11... | collective-permute-start | bytes 995336 | tf_op jit(solution)/shard_map/ppermute | solution.py:473

commit v5 on v4

--- a/solution.py
+++ b/solution.py
@@ -259,14 +259,15 @@
 
 def front_kernel(
     plan,
-    link_next_s, bond_next_v, other, lhs, k2_all, k3_all, gap2, gap3, bond_col, mine_h, vert_h,
-    ms, k2, k3, w2, w3,
-    w1, w2_first, mine, vert_s, sems,
+    charges_s, charges_v, other, lhs, k2_all, k3_all, gap2, gap3, bond_col, mine_h, vert_h,
+    ms, k2, k3, w2, w3_a, w3_b,
+    w1, w2_a, w2_b, mine, vert_s, sems,
 ):
     n, chi, half, lanes = plan.legs, plan.chi, plan.half, plan.lanes
     bf16 = jnp.bfloat16
     copies = fetch([(vert_h, vert_s), (mine_h, mine)], sems)
-    link_next = [link_next_s[0, i] for i in range(n)]
+    link_next = [charges_s[2, i] for i in range(n)]
+    bond_next = charges_v[0:1, :]
     tall = plan.pairs * plan.group_rows
     for r in range(n):
         at = slice(r * tall, (r + 1) * tall)
@@ -282,7 +283,7 @@
     copies[1].wait()
     for src, which in halves(mine, other):
         at = pl.multiple_of(which * half, 16)
-        gap = bond_next_v[...] - bond_col[pl.ds(at, half), :]
+        gap = bond_next - bond_col[pl.ds(at, half), :]
         for u in range(n):
             for v in range(n):
                 keep = gap == upper[u] - upper[v]
@@ -291,8 +292,9 @@
                 ms[u // 2, v // 2, pl.ds(at, half), lane : lane + chi] = val.astype(bf16)
     pad = n * plan.lm
     w1[:, :, pad:, :] = jnp.zeros((2, plan.pairs, plan.cols2 - pad, w1.shape[3]), bf16)
-    phases = [(o, vp, h) for o in range(2) for vp in range(plan.pairs) for h in range(2)]
+    phases = [(o, vp, h) for o in range(3) for vp in range(plan.pairs) for h in range(2)]
     per_g = plan.groups // (2 * plan.pairs)
+    chain, done = (w2_a, w2_b, w2), (w3_a, w3_b)
 
     def lead(o, vp, h):
         first(plan, quad_rows(lhs, plan, 2 * o + h), ms, w1.at[h], vp)
@@ -304,25 +306,44 @@
         if o:
             at = (2 * vp + h) * per_g
             for g in range(at, at + per_g):
-                third(plan, k3, w2_first, w3, g)
-        second(plan, k2, w1.at[h], w2 if o else w2_first, vp, h)
+                third(plan, k3, chain[o - 1], done[o - 1], g)
+        second(plan, k2, w1.at[h], chain[o], vp, h)
+
+
+def middle_kernel(plan, lhs, ms, k2, k3, w2_in, w2, w3, w1):
+    pad = plan.legs * plan.lm
+    w1[:, :, pad:, :] = jnp.zeros((2, plan.pairs, plan.cols2 - pad, w1.shape[3]), jnp.bfloat16)
+    phases = [(vp, h) for vp in range(plan.pairs) for h in range(2)]
+    per_g = plan.groups // len(phases)
+
+    def lead(vp, h):
+        first(plan, quad_rows(lhs, plan, 6 + h), ms, w1.at[h], vp)
+
+    lead(*phases[0])
+    for i, (vp, h) in enumerate(phases):
+        if i + 1 < len(phases):
+            lead(*phases[i + 1])
+        for g in range(i * per_g, (i + 1) * per_g):
+            third(plan, k3, w2_in, w3, g)
+        second(plan, k2, w1.at[h], w2, vp, h)
 
 
 def back_kernel(
     plan,
-    link_next_s,
-    bond_next_v, fresh_next_v, lhs, ms, k2, k3, w2_in, w3_in, pr_mine, pr_other,
-    image, partial, w2_odd, w3_even,
-    pr, w1, w2_even, w3_odd,
+    charges_s,
+    charges_v, lhs, ms, k2, k3, w2_in, w3_a, w3_b, w3_c, pr_mine, pr_other,
+    image, partial,
+    pr, w1, w2_a, w2_b, w3_d, w3_e, w3_f,
 ):
     n, chi, half, lanes = plan.legs, plan.chi, plan.half, plan.lanes
     bf16 = jnp.bfloat16
-    link_next = [link_next_s[0, i] for i in range(n)]
-    fresh_col = column_of(fresh_next_v[...])
+    link_next = [charges_s[2, i] for i in range(n)]
+    bond_next = charges_v[0:1, :]
+    fresh_col = column_of(charges_v[1:2, :])
     pr[...] = jnp.zeros_like(pr)
     for src, which in halves(pr_mine, pr_other):
         at = pl.multiple_of(which * half, 16)
-        gap = jnp.where(which == 0, fresh_col[:half], fresh_col[half:]) - bond_next_v[...]
+        gap = jnp.where(which == 0, fresh_col[:half], fresh_col[half:]) - bond_next
         for r in range(n):
             for s in range(n):
                 keep = gap == link_next[r] - link_next[s]
@@ -331,51 +352,54 @@
     pad = n * plan.lm
     w1[:, :, pad:, :] = jnp.zeros((2, plan.pairs, plan.cols2 - pad, w1.shape[3]), bf16)
 
-    del w2_in, w3_in
     block = 2 * QUAD * plan.xrows
     per_g = plan.groups // (2 * plan.pairs)
     per_r = n // (2 * plan.pairs)
-    w2, w3 = (w2_even, w2_odd), (w3_even, w3_odd)
 
     def put(oct, total):
-        image[pl.ds(pl.multiple_of(oct * block, 8), block), :] = total
+        image[oct * block : (oct + 1) * block, :] = total
         return jnp.sum(total * total)
 
-    def body(j, square_sum):
-        def lead(k, vp, h):
-            first(plan, quad_rows(lhs, plan, 2 * (2 * j + k + 2) + h), ms, w1.at[h], vp)
-
-        phases = [(k, vp, h) for k in range(2) for vp in range(plan.pairs) for h in range(2)]
+    w2 = (w2_in, w2_a, w2_b)
+    w3 = (w3_a, w3_b, w3_c, w3_d, w3_e, w3_f)
+    phases = [(o, vp, h) for o in range(2) for vp in range(plan.pairs) for h in range(2)]
+
+    def lead(o, vp, h):
+        first(plan, quad_rows(lhs, plan, 2 * (o + 4) + h), ms, w1.at[h], vp)
+
+    square_sum = 0.0
+    total = None
+    lead(*phases[0])
+    for i, (o, vp, h) in enumerate(phases):
+        if i + 1 < len(phases):
+            lead(*phases[i + 1])
+        phase = 2 * vp + h
+        for g in range(phase * per_g, (phase + 1) * per_g):
+            third(plan, k3, w2[o], w3[o + 3], g)
+        for r in range(phase * per_r, (phase + 1) * per_r):
+            total = add(total, fourth(w3[o], pr, r))
+        second(plan, k2, w1.at[h], w2[o + 1], vp, h)
+        if phase == 2 * plan.pairs - 1:
+            square_sum = square_sum + put(o, total)
+            total = None
+    partial[...] = jnp.full_like(partial, square_sum)
+
+    @pl.when(lax.axis_index("sec") >= 0)
+    def _():
+        square_sum = 0.0
         total = None
-        lead(*phases[0])
-        for i, (k, vp, h) in enumerate(phases):
-            if i + 1 < len(phases):
-                lead(*phases[i + 1])
-            phase = 2 * vp + h
-            for g in range(phase * per_g, (phase + 1) * per_g):
-                third(plan, k3, w2[1 - k], w3[1 - k], g)
-            for r in range(phase * per_r, (phase + 1) * per_r):
-                total = add(total, fourth(w3[k], pr, r))
-            second(plan, k2, w1.at[h], w2[k], vp, h)
-            if phase == 2 * plan.pairs - 1:
-                square_sum = square_sum + put(2 * j + k, total)
-                total = None
-        return square_sum
-
-    octs = half // (2 * QUAD)
-    square_sum = lax.fori_loop(0, (octs - 2) // 2, body, jnp.float32(0.0))
-    total = None
-    for g in range(plan.groups):
-        third(plan, k3, w2_odd, w3_odd, g)
-        if g % plan.pairs == 0:
-            total = add(total, fourth(w3_even, pr, g // plan.pairs))
-    square_sum = square_sum + put(octs - 2, total)
-    even = odd = None
-    for r in range(0, n, 2):
-        even = add(even, fourth(w3_odd, pr, r))
-        odd = add(odd, fourth(w3_odd, pr, r + 1))
-    square_sum = square_sum + put(octs - 1, even + odd)
-    partial[...] = jnp.full_like(partial, square_sum)
+        for g in range(plan.groups):
+            third(plan, k3, w2[2], w3[5], g)
+            if g % plan.pairs == 0:
+                total = add(total, fourth(w3[2], pr, g // plan.pairs))
+        square_sum = square_sum + put(2, total)
+        for o in range(3, 6):
+            even = odd = None
+            for r in range(0, n, 2):
+                even = add(even, fourth(w3[o], pr, r))
+                odd = add(odd, fourth(w3[o], pr, r + 1))
+            square_sum = square_sum + put(o, even + odd)
+        partial[...] += jnp.full_like(partial, square_sum)
 
 
 def finish_kernel(plan, count, columns, incoming, image, new, log_norm):
@@ -408,11 +432,11 @@
     smem, vmem = pltpu.SMEM, pltpu.VMEM
     swap = [(i, 1 - i) for i in range(sections)]
     hbm = pltpu.HBM
-    bond_next, fresh_next, link_next = from_behind((bond_charge, new_charge, link_charge), "col", -1)
+    link_row = jnp.pad(link_charge, ((0, 0), (0, chi - legs)))
+    charges = from_behind(jnp.concatenate([bond_charge, new_charge, link_row], axis=0), "col", -1)
     mine = jnp.transpose(mps[0], (1, 2, 0, 3)).reshape(squared, half, chi)
     other = lax.ppermute(mine, "sec", swap)
     pr_mine = from_behind(jnp.transpose(right_proj[0], (1, 2, 3, 0)).reshape(squared, half, chi), "col", -1)
-    bond_next, fresh_next, link_next = lax.optimization_barrier((bond_next, fresh_next, link_next))
     left = jnp.transpose(left_proj[0], (2, 3, 0, 1)).reshape(squared, half, chi)
     flat_ket = jnp.transpose(ket[0], (0, 1, 2, 4, 3)).reshape(squared, squared * phys)
     fetched = [left, bond_charge, new_charge, link_charge, vert_charge] + plan.matrices() + plan.indices()
@@ -437,7 +461,7 @@
         name="prep",
     )(flat_ket, *[pltpu.with_memory_space_constraint(x, pltpu.HBM) for x in fetched])
     octs = half // (2 * QUAD)
-    if half % (2 * QUAD) or octs % 2 or (QUAD * chi) % LANES:
+    if half % (2 * QUAD) or octs != 6 or (QUAD * chi) % LANES:
         raise ValueError("half")
     block = 2 * QUAD * plan.xrows
     lanes = plan.lanes
@@ -445,21 +469,23 @@
     w1_shape = (2, plan.pairs, plan.cols2, wide)
     w2_shape = jax.ShapeDtypeStruct((plan.groups, plan.cols3, wide), bf16)
     w3_shape = jax.ShapeDtypeStruct((legs, block, legs * lanes), bf16)
-    operands = [link_next, bond_next, other, lhs] + kets
+    operands = [charges, charges, other, lhs] + kets
     operands += [pltpu.with_memory_space_constraint(x, pltpu.HBM) for x in (mine, vert_charge)]
-    ms, k2, k3, w2, w3 = pl.pallas_call(
+    ms, k2, k3, w2, *w3 = pl.pallas_call(
         functools.partial(front_kernel, plan),
         in_specs=whole(smem, 1) + whole(vmem, len(operands) - 3) + whole(hbm, 2),
-        out_specs=whole(vmem, 5),
+        out_specs=whole(vmem, 6),
         out_shape=[
             jax.ShapeDtypeStruct((plan.pairs, plan.pairs, chi, 4 * lanes), bf16),
             jax.ShapeDtypeStruct((plan.rows2, plan.cols2), bf16),
             jax.ShapeDtypeStruct((plan.rows3, plan.cols3), bf16),
             w2_shape,
             w3_shape,
+            w3_shape,
         ],
         scratch_shapes=[
             pltpu.VMEM(w1_shape, bf16),
+            pltpu.VMEM(w2_shape.shape, bf16),
             pltpu.VMEM(w2_shape.shape, bf16),
             pltpu.VMEM(mine.shape, bf16),
             pltpu.SMEM(vert_charge.shape, jnp.int32),
@@ -469,26 +495,33 @@
         cost_estimate=pl.CostEstimate(flops=FRONT_FLOPS, bytes_accessed=1 << 20, transcendentals=0),
         name="front",
     )(*operands)
-    pr_mine, w3 = lax.optimization_barrier((pr_mine, w3))
+    pr_mine, w2 = lax.optimization_barrier((pr_mine, w2))
     pr_other = lax.ppermute(pr_mine, "sec", swap)
-    operands = [link_next, bond_next, fresh_next, lhs, ms, k2, k3, w2, w3, pr_mine, pr_other]
-    image, partial, _, _ = pl.pallas_call(
+    w2, w3_last = pl.pallas_call(
+        functools.partial(middle_kernel, plan),
+        in_specs=whole(vmem, 5),
+        out_specs=whole(vmem, 2),
+        out_shape=[w2_shape, w3_shape],
+        scratch_shapes=[pltpu.VMEM(w1_shape, bf16)],
+        compiler_params=pltpu.CompilerParams(vmem_limit_bytes=20 << 20),
+        cost_estimate=pl.CostEstimate(flops=FRONT_FLOPS, bytes_accessed=1 << 20, transcendentals=0),
+        name="middle",
+    )(lhs, ms, k2, k3, w2)
+    operands = [charges, charges, lhs, ms, k2, k3, w2, *w3, w3_last, pr_mine, pr_other]
+    image, partial = pl.pallas_call(
         functools.partial(back_kernel, plan),
         in_specs=whole(smem, 1) + whole(vmem, len(operands) - 1),
-        out_specs=whole(vmem, 4),
+        out_specs=whole(vmem, 2),
         out_shape=[
             jax.ShapeDtypeStruct((octs * block, chi), f32),
             jax.ShapeDtypeStruct((columns * sections, 1, LANES), f32),
-            w2_shape,
-            w3_shape,
         ],
-        input_output_aliases={7: 2, 8: 3},
         scratch_shapes=[
             pltpu.VMEM((legs, chi, legs * lanes), bf16),
             pltpu.VMEM(w1_shape, bf16),
-            pltpu.VMEM(w2_shape.shape, bf16),
-            pltpu.VMEM(w3_shape.shape, bf16),
-        ],
+        ]
+        + [pltpu.VMEM(w2_shape.shape, bf16)] * 2
+        + [pltpu.VMEM(w3_shape.shape, bf16)] * 3,
         compiler_params=pltpu.CompilerParams(vmem_limit_bytes=VMEM_LIMIT),
         cost_estimate=pl.CostEstimate(flops=2 * FRONT_FLOPS, bytes_accessed=1 << 20, transcendentals=0),
         name="back",

time: 61 us -> 58.8 us (0.964)
  starting transfers between devices: 9.67 us -> 7.74 us
  other arithmetic: 0 us -> 0.7 us
    pallas_call x1, Pallas kernels: 19.4 us -> 13.4 us  [absorb_row(): pl.pallas_call(functools.partial(back_kernel, plan), in_specs=whole(smem,...]
    pallas_call x0 -> x1, Pallas kernels: none -> 2.82 us  [absorb_row(): pl.pallas_call(functools.partial(middle_kernel, plan), in_specs=whole(vme...]
    pallas_call x1, Pallas kernels: 6.74 us -> 9.37 us  [absorb_row(): pl.pallas_call(functools.partial(front_kernel, plan), in_specs=whole(smem...]
    ppermute x4 -> x2, starting transfers between devices: 9.04 us -> 7.11 us  [from_behind(): return lax.ppermute(x, axis, [(i, (i + by) % count) for i in range(count)])]
    ppermute x1, waiting for transfers between devices: 1.78 us -> 0.01 us  [absorb_row(): pr_other = lax.ppermute(pr_mine, 'sec', swap)]
    ppermute x4 -> x2, waiting for transfers between devices: 4.77 us -> 6.01 us  [from_behind(): return lax.ppermute(x, axis, [(i, (i + by) % count) for i in range(count)])]
    concatenate x0 -> x1, other arithmetic: none -> 0.7 us  [absorb_row(): jnp.concatenate([bond_charge, new_charge, link_row], axis=0)]
  transfers between devices with their start and end apart: 6 -> 4, of which waited for: 2 -> 1; matrix products, arithmetic and copies ran while one was open for 2% -> 3% of each run, Pallas kernels for 14% -> 24%
where the time goes in v5:
time: 58.8 us; the launch traced here: 58.6 us
  Pallas kernels  28.8 us (49%)
  blocking collectives  13.4 us (23%)
  starting transfers between devices  7.74 us (13%)
  waiting for transfers between devices  6.02 us (10%)
  local copies, waits for them, and re-layouts  1.04 us (2%)
  between operations  0.85 us (1%)
  other arithmetic  0.7 us (1%)
    all_to_all x1, blocking collectives, absorb_row(): incoming = lax.all_to_all(partial, ('col', 'sec'), 0, 0, tiled=True)  13.4 us
    pallas_call x1, Pallas kernels, absorb_row(): pl.pallas_call(functools.partial(back_kernel, plan), in_specs=whole(smem,...  13.4 us
    pallas_call x1, Pallas kernels, absorb_row(): pl.pallas_call(functools.partial(front_kernel, plan), in_specs=whole(smem...  9.37 us
    ppermute x2, starting transfers between devices, from_behind(): return lax.ppermute(x, axis, [(i, (i + by) % count) for i in range(count)])  7.11 us
    ppermute x2, waiting for transfers between devices, from_behind(): return lax.ppermute(x, axis, [(i, (i + by) % count) for i in range(count)])  6.01 us
    pallas_call x1, Pallas kernels, absorb_row(): pl.pallas_call(functools.partial(middle_kernel, plan), in_specs=whole(vme...  2.82 us
    pallas_call x1, Pallas kernels, absorb_row(): pl.pallas_call(functools.partial(prep_kernel, plan), in_specs=whole(vmem,...  2.04 us
  transfers between devices with their start and end apart: 4, of which 1 were waited for; matrix products, arithmetic and copies ran while one was open for 3% of the time, Pallas kernels for 24%

profile of v5, /device:TPU:0, one launch (start us, length us, event | category | flops | bytes accessed | tf_op | source)
XLA Modules:
  0.0 58.6 jit_solution(4310667273325637894)
XLA Ops:
  0.6 0.6 collective-permute-start.1
  1.2 6.5 %collective-permute-start.2 = (bf16[36,48,96]{2,1,0:T(8,128)(2,1)}, bf16[36,48,96]{2,1,0:T(8,128)(2,1)S(1)}, u32[]{:S(2)}, u32[]{:S(2)}) collective-permute-start(bf16[36,48,96]{2,1,0:T(8,128)(2,1)} %bitcast.30), channel_id=1, source_target_pairs={{0,30},{2,0},{4,2},{6,4},{8,6},{10,8},{12,10},{14,12},{16,14},{18,... | collective-permute-start | bytes 995336 | tf_op jit(solution)/shard_map/ppermute | solution.py:23
  7.7 0.7 %pad_add_fusion = s32[3,96]{1,0:T(4,128)S(1)} fusion(s32[1,6]{1,0:T(1,128)} %link_h.1, s32[1,96]{1,0:T(1,128)} %fresh_h.1, s32[1,96]{1,0:T(1,128)} %bond_h.1), kind=kLoop, calls=%fused_computation | loop fusion | flops 576 | bytes 1944 | tf_op jit(solution)/shard_map/concatenate | solution.py:436
  8.4 0.6 collective-permute-start
  9.0 1.0 %reshape.25.ket = bf16[36,72]{1,0:T(8,128)(2,1)S(1)} reshape(bf16[6,6,6,2,6]{4,3,2,1,0:T(2,128)(2,1)} %bitcast.27) | data formatting | bytes 10368 | tf_op jit(solution)/shard_map/reshape | solution.py:441
  10.0 2.0 %prep.1 = (bf16[1920,96]{1,0:T(8,128)(2,1)S(1)}, bf16[432,256]{1,0:T(8,128)(2,1)S(1)}, bf16[96,144]{1,0:T(8,128)(2,1)S(1)}, s32[72,256]{1,0:T(8,128)S(1)}, s32[16,144]{1,0:T(8,128)S(1)}, /*index=5*/s32[96,1]{1,0:T(8,128)S(1)}) custom-call(bf16[36,72]{1,0:T(8,128)(2,1)S(1)} %reshape.25.ket, bf16[36,48,96]{2,1,0:T(8,128)(2,1)} %bitcast.26, s32[1,96]{1,0:T(1,128)} %bond_h.1, ...), custom_call_target="tpu_custom_call" | custom-call | flops 134217728 | bytes 1048576 | tf_op jit(solution)/shard_map/prep/pallas_call | solution.py:446
  12.1 6.0 %collective-permute-done.charges_s.charges_v = s32[3,96]{1,0:T(4,128)S(1)} collective-permute-done((s32[3,96]{1,0:T(4,128)S(1)}, s32[3,96]{1,0:T(4,128)S(1)}, u32[]{:S(2)}, u32[]{:S(2)}) %collective-permute-start) | collective-permute-done | bytes 1184 | tf_op jit(solution)/shard_map/ppermute | solution.py:23
  18.1 0.0 collective-permute-done.1.other
  18.1 9.4 %front.1 = (bf16[3,3,96,512]{3,2,1,0:T(8,128)(2,1)S(1)}, bf16[432,256]{1,0:T(8,128)(2,1)S(1)}, bf16[96,144]{1,0:T(8,128)(2,1)S(1)}, bf16[18,144,768]{2,1,0:T(8,1...) custom-call(s32[3,96]{1,0:T(4,128)S(1)} %collective-permute-done.charges_s.charges_v, ...), custom_call_target="tpu_custom_call" | custom-call | flops 1073741824 | bytes 1048576 | tf_op jit(solution)/shard_map/front/pallas_call | solution.py:474
  27.5 0.0 collective-permute-done.2.pr_mine
  27.5 0.1 collective-permute-start.3
  27.6 2.8 %middle.1 = (bf16[18,144,768]{2,1,0:T(8,128)(2,1)S(1)}, bf16[6,384,768]{2,1,0:T(8,128)(2,1)S(1)}) custom-call(bf16[1920,96]{1,0:T(8,128)(2,1)S(1)} %get-tuple-element.22.lhs, bf16[3,3,96,512]{3,2,1,0:T(8,128)(2,1)S(1)} %get-tuple-element.28.ms, bf16[432,256]{1,0:T(8,128)(2,1)S(1)} %get-tuple-element.29.k2, bf16[96,144]{1,0:T(8,128)(2,1)S(1)} %get-tuple-element.30.k3, ...), custom_call_target="tpu_custom_call" | custom-call | flops 1073741824 | bytes 1048576 | tf_op jit(solution)/shard_map/middle/pallas_call | solution.py:500
  30.4 0.0 collective-permute-done.3.pr_other
  30.4 13.4 %back.1 = (f32[2304,96]{1,0:T(8,128)S(1)}, f32[32,1,128]{2,1,0:T(1,128)S(1)}) custom-call(s32[3,96]{1,0:T(4,128)S(1)} %collective-permute-done.charges_s.charges_v, s32[3,96]{1,0:T(4,128)S(1)} %collective-permute-done.charges_s.charges_v, bf16[1920,96]{1,0:T(8,128)(2,1)S(1)} %get-tuple-element.22.lhs, bf16[3,3,96,512]{3,2,1,0:T(8,128)(2,1)S(1)} %get-tuple-element.28.ms, ...), custom_call_target="tpu_custom_call" | custom-call | flops 2147483648 | bytes 1048576 | tf_op jit(solution)/shard_map/back/pallas_call | solution.py:511
  43.8 13.4 %all_to_all.5 = f32[32,1,128]{2,1,0:T(1,128)S(1)} all-to-all(f32[32,1,128]{2,1,0:T(1,128)S(1)} %get-tuple-element.38), channel_id=1, replica_groups=mesh['col'=16,'sec'=2] {'col','sec'}, dimensions={0} | all-to-all | bytes 32768 | tf_op jit(solution)/shard_map/all_to_all | solution.py:529
  57.3 1.1 %finish.1 = (bf16[36,48,96]{2,1,0:T(8,128)(2,1)}, f32[1,1]{1,0:T(1,128)}) custom-call(f32[32,128]{1,0:T(8,128)S(1)} %bitcast.25, f32[2304,96]{1,0:T(8,128)S(1)} %get-tuple-element.39.image), custom_call_target="tpu_custom_call" | custom-call | tf_op jit(solution)/shard_map/finish/pallas_call | solution.py:530
Async XLA Ops:
  0.6 17.5 %collective-permute-start.1 = (bf16[36,48,96]{2,1,0:T(8,128)(2,1)}, bf16[36,48,96]{2,1,0:T(8,128)(2,1)S(1)}, u32[]{:S(2)}, u32[]{:S(2)}) collective-permute-start(bf16[36,48,96]{2,1,0:T(8,128)(2,1)} %bitcast.28), channel_id=1, source_target_pairs={{0,1},{1,0},{2,3},{3,2},{4,5},{5,4},{6,7},{7,6},{8,9},{9,8},{10,11... | collective-permute-start | bytes 995336 | tf_op jit(solution)/shard_map/ppermute | solution.py:438
  1.2 26.3 %collective-permute-start.2 = (bf16[36,48,96]{2,1,0:T(8,128)(2,1)}, bf16[36,48,96]{2,1,0:T(8,128)(2,1)S(1)}, u32[]{:S(2)}, u32[]{:S(2)}) collective-permute-start(bf16[36,48,96]{2,1,0:T(8,128)(2,1)} %bitcast.30), channel_id=1, source_target_pairs={{0,30},{2,0},{4,2},{6,4},{8,6},{10,8},{12,10},{14,12},{16,14},{18,... | collective-permute-start | bytes 995336 | tf_op jit(solution)/shard_map/ppermute | solution.py:23
  8.4 9.7 %collective-permute-start = (s32[3,96]{1,0:T(4,128)S(1)}, s32[3,96]{1,0:T(4,128)S(1)}, u32[]{:S(2)}, u32[]{:S(2)}) collective-permute-start(s32[3,96]{1,0:T(4,128)S(1)} %pad_add_fusion), channel_id=1, source_target_pairs={{0,30},{2,0},{4,2},{6,4},{8,6},{10,8},{12,10},{14,12},{16,14},{18,... | collective-permute-start | bytes 3464 | tf_op jit(solution)/shard_map/ppermute | solution.py:23
  27.5 2.9 %collective-permute-start.3 = (bf16[36,48,96]{2,1,0:T(8,128)(2,1)S(1)}, bf16[36,48,96]{2,1,0:T(8,128)(2,1)S(1)}, u32[]{:S(2)}, u32[]{:S(2)}) collective-permute-start(bf16[36,48,96]{2,1,0:T(8,128)(2,1)S(1)} %collective-permute-done.2.pr_mine), channel_id=1, source_target_pairs={{0,1},{1,0},{2,3},{3,2},{4,5},{5,4},{6,7},{7,6},{8,9},{9,8},{10,11... | collective-permute-start | bytes 995336 | tf_op jit(solution)/shard_map/ppermute | solution.py:499

commit v6 on v5

--- a/solution.py
+++ b/solution.py
@@ -33,8 +33,8 @@
         self.groups = legs * self.pairs
         self.rows2 = self.groups * self.group_rows
         self.cols2 = round_up(legs * self.lm, 256)
-        self.seg = round_up(2 * legs, 16)
-        self.rows3 = legs * self.seg
+        self.seg = 2 * legs
+        self.rows3 = round_up(legs * self.seg, 16)
         self.cols3 = legs * self.group_rows
         self.xrows = self.pairs * self.seg
 
@@ -83,13 +83,13 @@
 
     def indices(self):
         n, ph = self.legs, self.phys
-        rows = np.zeros((n * n * ph, 8), np.int32)
+        rows = np.zeros((max(n * n * ph, self.rows3), 8), np.int32)
         cols = np.zeros((8, self.cols2), np.int32)
         for i in range(n * n * ph):
             rest = i % self.group_rows
             rows[i, 0] = i // self.group_rows * 2 + rest // (n * ph)
             rows[i, 1] = rest % ph
-        for i in range(self.seg):
+        for i in range(self.rows3):
             rows[i, 2] = i % n
         for u in range(n):
             for i in range(n * n):
@@ -164,9 +164,10 @@
     for p in range(1, plan.phys):
         total = total + expand(r3[p], c3[p])
     k3[...] = (total * m3[...].astype(jnp.float32)).astype(jnp.bfloat16)
-    rows_d = look_up(rows[:, 0:1], lower) + rows[:, 1:2]
+    tall = n * n * plan.phys
+    rows_d = look_up(rows[:tall, 0:1], lower) + rows[:tall, 1:2]
     gap2[...] = look_up(cols[0:1, :], upper) + look_up(cols[1:2, :], link) - rows_d
-    rows_e = look_up(rows[: plan.seg, 2:3], lower)
+    rows_e = look_up(rows[: plan.rows3, 2:3], lower)
     c = slice(0, plan.cols3)
     gap3[...] = look_up(cols[2:3, c], upper) + look_up(cols[3:4, c], link) - cols[4:5, c] - rows_e
 
@@ -235,13 +236,14 @@
     r, dp = g // plan.pairs, g % plan.pairs
     out = dot(k3[...], w2[g])
     per = QUAD * plan.chi // LANES
+    quad = QUAD * plan.xrows
     for h in range(2):
         tiles = [out[:, t * LANES : (t + 1) * LANES] for t in range(h * per, (h + 1) * per)]
-        for x, part in enumerate(unpack_lanes(tiles, plan.chi, QUAD)):
-            part = part.astype(jnp.bfloat16)
-            at = (h * QUAD + x) * plan.xrows + dp * seg
-            for s in range(plan.legs):
-                w3[r, at : at + seg, s * LANES : (s + 1) * LANES] = part[s * seg : (s + 1) * seg]
+        parts = unpack_lanes(tiles, plan.chi, QUAD)
+        at = h * quad + dp * QUAD * seg
+        for s in range(plan.legs):
+            stacked = jnp.concatenate([part[s * seg : (s + 1) * seg] for part in parts], axis=0)
+            w3[r, at : at + QUAD * seg, s * LANES : (s + 1) * LANES] = stacked.astype(jnp.bfloat16)
 
 
 def fourth(w3, pr, r):
@@ -272,8 +274,11 @@
     for r in range(n):
         at = slice(r * tall, (r + 1) * tall)
         k2[at] = jnp.where(gap2[...] == link_next[r], k2_all[at].astype(jnp.float32), 0.0).astype(bf16)
-        at = slice(r * plan.seg, (r + 1) * plan.seg)
-        k3[at] = jnp.where(gap3[...] == link_next[r], k3_all[at].astype(jnp.float32), 0.0).astype(bf16)
+    row = lax.broadcasted_iota(jnp.int32, gap3.shape, 0)
+    link_rows = jnp.zeros(gap3.shape, jnp.int32)
+    for s in range(n):
+        link_rows = jnp.where(row >= s * plan.seg, link_next[s], link_rows)
+    k3[...] = jnp.where(gap3[...] == link_rows, k3_all[...].astype(jnp.float32), 0.0).astype(bf16)
     if chi < lanes:
         for k in range(4):
             at = slice(k * lanes + chi, (k + 1) * lanes)
@@ -357,7 +362,13 @@
     per_r = n // (2 * plan.pairs)
 
     def put(oct, total):
-        image[oct * block : (oct + 1) * block, :] = total
+        pieces = []
+        for h in range(2):
+            for x in range(QUAD):
+                for dp in range(plan.pairs):
+                    at = ((h * plan.pairs + dp) * QUAD + x) * plan.seg
+                    pieces.append(total[at : at + plan.seg])
+        image[oct * block : (oct + 1) * block, :] = jnp.concatenate(pieces, axis=0)
         return jnp.sum(total * total)
 
     w2 = (w2_in, w2_a, w2_b)
@@ -452,7 +463,7 @@
             jax.ShapeDtypeStruct((plan.rows2, plan.cols2), bf16),
             jax.ShapeDtypeStruct((plan.rows3, plan.cols3), bf16),
             jax.ShapeDtypeStruct((squared * phys, plan.cols2), jnp.int32),
-            jax.ShapeDtypeStruct((plan.seg, plan.cols3), jnp.int32),
+            jax.ShapeDtypeStruct((plan.rows3, plan.cols3), jnp.int32),
             jax.ShapeDtypeStruct((chi, 1), jnp.int32),
         ],
         scratch_shapes=[pltpu.VMEM((half * plan.lm, chi), f32)] + scratch + [pltpu.SemaphoreType.DMA((len(fetched),))],
@@ -461,7 +472,7 @@
         name="prep",
     )(flat_ket, *[pltpu.with_memory_space_constraint(x, pltpu.HBM) for x in fetched])
     octs = half // (2 * QUAD)
-    if half % (2 * QUAD) or octs != 6 or (QUAD * chi) % LANES:
+    if half % (2 * QUAD) or octs != 6 or (QUAD * chi) % LANES or QUAD * plan.seg % 16:
         raise ValueError("half")
     block = 2 * QUAD * plan.xrows
     lanes = plan.lanes

time: 58.8 us -> 57.3 us (0.974)
  Pallas kernels: 28.8 us -> 27.3 us
    pallas_call x1, Pallas kernels: 13.4 us -> 11.9 us  [absorb_row(): pl.pallas_call(functools.partial(back_kernel, plan), in_specs=whole(smem,...]
  transfers between devices with their start and end apart: 4 -> 4, of which waited for: 1 -> 1; matrix products, arithmetic and copies ran while one was open for 3% -> 3% of each run, Pallas kernels for 24% -> 25%
where the time goes in v6:
time: 57.3 us; the launch traced here: 57.1 us
  Pallas kernels  27.3 us (48%)
  blocking collectives  13.5 us (24%)
  starting transfers between devices  7.74 us (14%)
  waiting for transfers between devices  6.02 us (11%)
  local copies, waits for them, and re-layouts  1.04 us (2%)
  between operations  0.85 us (1%)
  other arithmetic  0.7 us (1%)
    all_to_all x1, blocking collectives, absorb_row(): incoming = lax.all_to_all(partial, ('col', 'sec'), 0, 0, tiled=True)  13.5 us
    pallas_call x1, Pallas kernels, absorb_row(): pl.pallas_call(functools.partial(back_kernel, plan), in_specs=whole(smem,...  11.9 us
    pallas_call x1, Pallas kernels, absorb_row(): pl.pallas_call(functools.partial(front_kernel, plan), in_specs=whole(smem...  9.61 us
    ppermute x2, starting transfers between devices, from_behind(): return lax.ppermute(x, axis, [(i, (i + by) % count) for i in range(count)])  7.11 us
    ppermute x2, waiting for transfers between devices, from_behind(): return lax.ppermute(x, axis, [(i, (i + by) % count) for i in range(count)])  6.02 us
    pallas_call x1, Pallas kernels, absorb_row(): pl.pallas_call(functools.partial(middle_kernel, plan), in_specs=whole(vme...  2.84 us
    pallas_call x1, Pallas kernels, absorb_row(): pl.pallas_call(functools.partial(prep_kernel, plan), in_specs=whole(vmem,...  2.04 us
  transfers between devices with their start and end apart: 4, of which 1 were waited for; matrix products, arithmetic and copies ran while one was open for 3% of the time, Pallas kernels for 25%

profile of v6, /device:TPU:0, one launch (start us, length us, event | category | flops | bytes accessed | tf_op | source)
XLA Modules:
  0.0 57.1 jit_solution(12115934260058480781)
XLA Ops:
  0.6 0.6 collective-permute-start.1
  1.2 6.5 %collective-permute-start.2 = (bf16[36,48,96]{2,1,0:T(8,128)(2,1)}, bf16[36,48,96]{2,1,0:T(8,128)(2,1)S(1)}, u32[]{:S(2)}, u32[]{:S(2)}) collective-permute-start(bf16[36,48,96]{2,1,0:T(8,128)(2,1)} %bitcast.30), channel_id=1, source_target_pairs={{0,30},{2,0},{4,2},{6,4},{8,6},{10,8},{12,10},{14,12},{16,14},{18,... | collective-permute-start | bytes 995336 | tf_op jit(solution)/shard_map/ppermute | solution.py:23
  7.7 0.7 %pad_add_fusion = s32[3,96]{1,0:T(4,128)S(1)} fusion(s32[1,6]{1,0:T(1,128)} %link_h.1, s32[1,96]{1,0:T(1,128)} %fresh_h.1, s32[1,96]{1,0:T(1,128)} %bond_h.1), kind=kLoop, calls=%fused_computation | loop fusion | flops 576 | bytes 1944 | tf_op jit(solution)/shard_map/concatenate | solution.py:447
  8.4 0.6 %collective-permute-start = (s32[3,96]{1,0:T(4,128)S(1)}, s32[3,96]{1,0:T(4,128)S(1)}, u32[]{:S(2)}, u32[]{:S(2)}) collective-permute-start(s32[3,96]{1,0:T(4,128)S(1)} %pad_add_fusion), channel_id=1, source_target_pairs={{0,30},{2,0},{4,2},{6,4},{8,6},{10,8},{12,10},{14,12},{16,14},{18,... | collective-permute-start | bytes 3464 | tf_op jit(solution)/shard_map/ppermute | solution.py:23
  9.0 1.0 %reshape.25.ket = bf16[36,72]{1,0:T(8,128)(2,1)S(1)} reshape(bf16[6,6,6,2,6]{4,3,2,1,0:T(2,128)(2,1)} %bitcast.27) | data formatting | bytes 10368 | tf_op jit(solution)/shard_map/reshape | solution.py:452
  10.0 2.0 %prep.1 = (bf16[1920,96]{1,0:T(8,128)(2,1)S(1)}, bf16[432,256]{1,0:T(8,128)(2,1)S(1)}, bf16[80,144]{1,0:T(8,128)(2,1)S(1)}, s32[72,256]{1,0:T(8,128)S(1)}, s32[80,144]{1,0:T(8,128)S(1)}, /*index=5*/s32[96,1]{1,0:T(8,128)S(1)}) custom-call(bf16[36,72]{1,0:T(8,128)(2,1)S(1)} %reshape.25.ket, bf16[36,48,96]{2,1,0:T(8,128)(2,1)} %bitcast.26, s32[1,96]{1,0:T(1,128)} %bond_h.1, ...), custom_call_target="tpu_custom_call" | custom-call | flops 134217728 | bytes 1048576 | tf_op jit(solution)/shard_map/prep/pallas_call | solution.py:457
  12.1 6.0 %collective-permute-done.charges_s.charges_v = s32[3,96]{1,0:T(4,128)S(1)} collective-permute-done((s32[3,96]{1,0:T(4,128)S(1)}, s32[3,96]{1,0:T(4,128)S(1)}, u32[]{:S(2)}, u32[]{:S(2)}) %collective-permute-start) | collective-permute-done | bytes 1184 | tf_op jit(solution)/shard_map/ppermute | solution.py:23
  18.1 0.0 collective-permute-done.1.other
  18.1 9.6 %front.1 = (bf16[3,3,96,512]{3,2,1,0:T(8,128)(2,1)S(1)}, bf16[432,256]{1,0:T(8,128)(2,1)S(1)}, bf16[80,144]{1,0:T(8,128)(2,1)S(1)}, bf16[18,144,768]{2,1,0:T(8,1...) custom-call(s32[3,96]{1,0:T(4,128)S(1)} %collective-permute-done.charges_s.charges_v, ...), custom_call_target="tpu_custom_call" | custom-call | flops 1073741824 | bytes 1048576 | tf_op jit(solution)/shard_map/front/pallas_call | solution.py:485
  27.7 0.0 collective-permute-done.2.pr_mine
  27.7 0.1 collective-permute-start.3
  27.8 2.8 %middle.1 = (bf16[18,144,768]{2,1,0:T(8,128)(2,1)S(1)}, bf16[6,288,768]{2,1,0:T(8,128)(2,1)S(1)}) custom-call(bf16[1920,96]{1,0:T(8,128)(2,1)S(1)} %get-tuple-element.22.lhs, bf16[3,3,96,512]{3,2,1,0:T(8,128)(2,1)S(1)} %get-tuple-element.28.ms, bf16[432,256]{1,0:T(8,128)(2,1)S(1)} %get-tuple-element.29.k2, bf16[80,144]{1,0:T(8,128)(2,1)S(1)} %get-tuple-element.30.k3, ...), custom_call_target="tpu_custom_call" | custom-call | flops 1073741824 | bytes 1048576 | tf_op jit(solution)/shard_map/middle/pallas_call | solution.py:511
  30.7 0.0 collective-permute-done.3.pr_other
  30.7 11.9 %back.1 = (f32[1728,96]{1,0:T(8,128)S(1)}, f32[32,1,128]{2,1,0:T(1,128)S(1)}) custom-call(s32[3,96]{1,0:T(4,128)S(1)} %collective-permute-done.charges_s.charges_v, s32[3,96]{1,0:T(4,128)S(1)} %collective-permute-done.charges_s.charges_v, bf16[1920,96]{1,0:T(8,128)(2,1)S(1)} %get-tuple-element.22.lhs, bf16[3,3,96,512]{3,2,1,0:T(8,128)(2,1)S(1)} %get-tuple-element.28.ms, ...), custom_call_target="tpu_custom_call" | custom-call | flops 2147483648 | bytes 1048576 | tf_op jit(solution)/shard_map/back/pallas_call | solution.py:522
  42.6 13.5 %all_to_all.5 = f32[32,1,128]{2,1,0:T(1,128)S(1)} all-to-all(f32[32,1,128]{2,1,0:T(1,128)S(1)} %get-tuple-element.38), channel_id=1, replica_groups=mesh['col'=16,'sec'=2] {'col','sec'}, dimensions={0} | all-to-all | bytes 32768 | tf_op jit(solution)/shard_map/all_to_all | solution.py:540
  56.1 0.9 %finish.1 = (bf16[36,48,96]{2,1,0:T(8,128)(2,1)}, f32[1,1]{1,0:T(1,128)}) custom-call(f32[32,128]{1,0:T(8,128)S(1)} %bitcast.25, f32[1728,96]{1,0:T(8,128)S(1)} %get-tuple-element.39.image), custom_call_target="tpu_custom_call" | custom-call | tf_op jit(solution)/shard_map/finish/pallas_call | solution.py:541
Async XLA Ops:
  0.6 17.5 %collective-permute-start.1 = (bf16[36,48,96]{2,1,0:T(8,128)(2,1)}, bf16[36,48,96]{2,1,0:T(8,128)(2,1)S(1)}, u32[]{:S(2)}, u32[]{:S(2)}) collective-permute-start(bf16[36,48,96]{2,1,0:T(8,128)(2,1)} %bitcast.28), channel_id=1, source_target_pairs={{0,1},{1,0},{2,3},{3,2},{4,5},{5,4},{6,7},{7,6},{8,9},{9,8},{10,11... | collective-permute-start | bytes 995336 | tf_op jit(solution)/shard_map/ppermute | solution.py:449
  1.2 26.5 %collective-permute-start.2 = (bf16[36,48,96]{2,1,0:T(8,128)(2,1)}, bf16[36,48,96]{2,1,0:T(8,128)(2,1)S(1)}, u32[]{:S(2)}, u32[]{:S(2)}) collective-permute-start(bf16[36,48,96]{2,1,0:T(8,128)(2,1)} %bitcast.30), channel_id=1, source_target_pairs={{0,30},{2,0},{4,2},{6,4},{8,6},{10,8},{12,10},{14,12},{16,14},{18,... | collective-permute-start | bytes 995336 | tf_op jit(solution)/shard_map/ppermute | solution.py:23
  8.4 9.7 %collective-permute-start = (s32[3,96]{1,0:T(4,128)S(1)}, s32[3,96]{1,0:T(4,128)S(1)}, u32[]{:S(2)}, u32[]{:S(2)}) collective-permute-start(s32[3,96]{1,0:T(4,128)S(1)} %pad_add_fusion), channel_id=1, source_target_pairs={{0,30},{2,0},{4,2},{6,4},{8,6},{10,8},{12,10},{14,12},{16,14},{18,... | collective-permute-start | bytes 3464 | tf_op jit(solution)/shard_map/ppermute | solution.py:23
  27.7 2.9 %collective-permute-start.3 = (bf16[36,48,96]{2,1,0:T(8,128)(2,1)S(1)}, bf16[36,48,96]{2,1,0:T(8,128)(2,1)S(1)}, u32[]{:S(2)}, u32[]{:S(2)}) collective-permute-start(bf16[36,48,96]{2,1,0:T(8,128)(2,1)S(1)} %collective-permute-done.2.pr_mine), channel_id=1, source_target_pairs={{0,1},{1,0},{2,3},{3,2},{4,5},{5,4},{6,7},{7,6},{8,9},{9,8},{10,11... | collective-permute-start | bytes 995336 | tf_op jit(solution)/shard_map/ppermute | solution.py:510

commit v7 on v6

--- a/solution.py
+++ b/solution.py
@@ -126,13 +126,13 @@
 
 def prep_kernel(
     plan,
-    ket, left_h, bond_h, fresh_h, link_h, vert_h, r2_h, c2_h, m2_h, r3_h, c3_h, m3_h, rows_h, cols_h,
-    out, k2, k3, gap2, gap3, bond_col,
+    ket, left_h, bond_h, fresh_h, link_h, vert_h, r2_h, c2_h, m2_h, r3_h, c3_h, m3_h, rows_h, cols_h, mine_h,
+    out, k2, k3, gap2, gap3, bond_col, upper_rows, mine,
     wide, left, bond, fresh, link_s, vert_s, r2, c2, m2, r3, c3, m3, rows, cols, sems,
 ):
     n, half, lm = plan.legs, plan.half, plan.lm
-    sources = (link_h, vert_h, bond_h, fresh_h, left_h, r2_h, c2_h, m2_h, r3_h, c3_h, m3_h, rows_h, cols_h)
-    targets = (link_s, vert_s, bond, fresh, left, r2, c2, m2, r3, c3, m3, rows, cols)
+    sources = (link_h, vert_h, bond_h, fresh_h, left_h, r2_h, c2_h, m2_h, r3_h, c3_h, m3_h, rows_h, cols_h, mine_h)
+    targets = (link_s, vert_s, bond, fresh, left, r2, c2, m2, r3, c3, m3, rows, cols, mine)
     copies = fetch(list(zip(sources, targets)), sems)
     for row in range(n * n, lm):
         wide[pl.ds(row, half, stride=lm), :] = jnp.zeros((half, plan.chi), jnp.float32)
@@ -145,6 +145,8 @@
     fresh_all = column_of(fresh[...])
     fresh_col = jnp.where(sec == 0, fresh_all[:half], fresh_all[half:])
     bond_col[...] = column_of(bond[...])
+    for i in range(n):
+        upper_rows[i : i + 1, :] = jnp.full((1, plan.chi), upper[i], jnp.int32)
     gap = fresh_col - bond[...]
     for l in range(n):
         for m in range(n):
@@ -261,13 +263,12 @@
 
 def front_kernel(
     plan,
-    charges_s, charges_v, other, lhs, k2_all, k3_all, gap2, gap3, bond_col, mine_h, vert_h,
+    charges_s, charges_v, other, lhs, k2_all, k3_all, gap2, gap3, bond_col, upper_rows, mine,
     ms, k2, k3, w2, w3_a, w3_b,
-    w1, w2_a, w2_b, mine, vert_s, sems,
+    w1, w2_a, w2_b,
 ):
     n, chi, half, lanes = plan.legs, plan.chi, plan.half, plan.lanes
     bf16 = jnp.bfloat16
-    copies = fetch([(vert_h, vert_s), (mine_h, mine)], sems)
     link_next = [charges_s[2, i] for i in range(n)]
     bond_next = charges_v[0:1, :]
     tall = plan.pairs * plan.group_rows
@@ -283,9 +284,7 @@
         for k in range(4):
             at = slice(k * lanes + chi, (k + 1) * lanes)
             ms[:, :, :, at] = jnp.zeros((plan.pairs, plan.pairs, chi, lanes - chi), bf16)
-    copies[0].wait()
-    upper = [vert_s[0, 0, i] for i in range(n)]
-    copies[1].wait()
+    upper = [upper_rows[i : i + 1, :] for i in range(n)]
     for src, which in halves(mine, other):
         at = pl.multiple_of(which * half, 16)
         gap = bond_next - bond_col[pl.ds(at, half), :]
@@ -450,14 +449,13 @@
     pr_mine = from_behind(jnp.transpose(right_proj[0], (1, 2, 3, 0)).reshape(squared, half, chi), "col", -1)
     left = jnp.transpose(left_proj[0], (2, 3, 0, 1)).reshape(squared, half, chi)
     flat_ket = jnp.transpose(ket[0], (0, 1, 2, 4, 3)).reshape(squared, squared * phys)
-    fetched = [left, bond_charge, new_charge, link_charge, vert_charge] + plan.matrices() + plan.indices()
+    fetched = [left, bond_charge, new_charge, link_charge, vert_charge] + plan.matrices() + plan.indices() + [mine]
     in_smem = (3, 4)
-    scratch = [(smem if i in in_smem else vmem)(x.shape, x.dtype) for i, x in enumerate(fetched)]
-    scratch = [scratch[i] for i in (0, 1, 2, 3, 4)] + scratch[5:]
+    scratch = [(smem if i in in_smem else vmem)(x.shape, x.dtype) for i, x in enumerate(fetched[:-1])]
     lhs, *kets = pl.pallas_call(
         functools.partial(prep_kernel, plan),
         in_specs=whole(vmem, 1) + whole(hbm, len(fetched)),
-        out_specs=whole(vmem, 6),
+        out_specs=whole(vmem, 8),
         out_shape=[
             jax.ShapeDtypeStruct((half * plan.lm, chi), bf16),
             jax.ShapeDtypeStruct((plan.rows2, plan.cols2), bf16),
@@ -465,6 +463,8 @@
             jax.ShapeDtypeStruct((squared * phys, plan.cols2), jnp.int32),
             jax.ShapeDtypeStruct((plan.rows3, plan.cols3), jnp.int32),
             jax.ShapeDtypeStruct((chi, 1), jnp.int32),
+            jax.ShapeDtypeStruct((round_up(legs, 8), chi), jnp.int32),
+            jax.ShapeDtypeStruct(mine.shape, bf16),
         ],
         scratch_shapes=[pltpu.VMEM((half * plan.lm, chi), f32)] + scratch + [pltpu.SemaphoreType.DMA((len(fetched),))],
         compiler_params=pltpu.CompilerParams(vmem_limit_bytes=12 << 20),
@@ -481,10 +481,9 @@
     w2_shape = jax.ShapeDtypeStruct((plan.groups, plan.cols3, wide), bf16)
     w3_shape = jax.ShapeDtypeStruct((legs, block, legs * lanes), bf16)
     operands = [charges, charges, other, lhs] + kets
-    operands += [pltpu.with_memory_space_constraint(x, pltpu.HBM) for x in (mine, vert_charge)]
     ms, k2, k3, w2, *w3 = pl.pallas_call(
         functools.partial(front_kernel, plan),
-        in_specs=whole(smem, 1) + whole(vmem, len(operands) - 3) + whole(hbm, 2),
+        in_specs=whole(smem, 1) + whole(vmem, len(operands) - 1),
         out_specs=whole(vmem, 6),
         out_shape=[
             jax.ShapeDtypeStruct((plan.pairs, plan.pairs, chi, 4 * lanes), bf16),
@@ -498,9 +497,6 @@
             pltpu.VMEM(w1_shape, bf16),
             pltpu.VMEM(w2_shape.shape, bf16),
             pltpu.VMEM(w2_shape.shape, bf16),
-            pltpu.VMEM(mine.shape, bf16),
-            pltpu.SMEM(vert_charge.shape, jnp.int32),
-            pltpu.SemaphoreType.DMA((2,)),
         ],
         compiler_params=pltpu.CompilerParams(vmem_limit_bytes=VMEM_LIMIT),
         cost_estimate=pl.CostEstimate(flops=FRONT_FLOPS, bytes_accessed=1 << 20, transcendentals=0),

time: 57.3 us -> 55.8 us (0.974)
  Pallas kernels: 27.3 us -> 25.9 us
    pallas_call x1, Pallas kernels: 9.61 us -> 8.49 us  [absorb_row(): pl.pallas_call(functools.partial(front_kernel, plan), in_specs=whole(smem...]
  transfers between devices with their start and end apart: 4 -> 4, of which waited for: 1 -> 1; matrix products, arithmetic and copies ran while one was open for 3% -> 3% of each run, Pallas kernels for 25% -> 24%
where the time goes in v7:
time: 55.8 us; the launch traced here: 55.6 us
  Pallas kernels  25.9 us (46%)
  blocking collectives  13.4 us (24%)
  starting transfers between devices  7.74 us (14%)
  waiting for transfers between devices  6.01 us (11%)
  local copies, waits for them, and re-layouts  1.04 us (2%)
  between operations  0.85 us (2%)
  other arithmetic  0.7 us (1%)
    all_to_all x1, blocking collectives, absorb_row(): incoming = lax.all_to_all(partial, ('col', 'sec'), 0, 0, tiled=True)  13.4 us
    pallas_call x1, Pallas kernels, absorb_row(): pl.pallas_call(functools.partial(back_kernel, plan), in_specs=whole(smem,...  11.7 us
    pallas_call x1, Pallas kernels, absorb_row(): pl.pallas_call(functools.partial(front_kernel, plan), in_specs=whole(smem...  8.49 us
    ppermute x2, starting transfers between devices, from_behind(): return lax.ppermute(x, axis, [(i, (i + by) % count) for i in range(count)])  7.11 us
    ppermute x2, waiting for transfers between devices, from_behind(): return lax.ppermute(x, axis, [(i, (i + by) % count) for i in range(count)])  6 us
    pallas_call x1, Pallas kernels, absorb_row(): pl.pallas_call(functools.partial(middle_kernel, plan), in_specs=whole(vme...  2.76 us
    pallas_call x1, Pallas kernels, absorb_row(): pl.pallas_call(functools.partial(prep_kernel, plan), in_specs=whole(vmem,...  2.05 us
  transfers between devices with their start and end apart: 4, of which 1 were waited for; matrix products, arithmetic and copies ran while one was open for 3% of the time, Pallas kernels for 24%

profile of v7, /device:TPU:0, one launch (start us, length us, event | category | flops | bytes accessed | tf_op | source)
XLA Modules:
  0.0 55.6 jit_solution(9064404890246526253)
XLA Ops:
  0.6 0.6 %collective-permute-start.1 = (bf16[36,48,96]{2,1,0:T(8,128)(2,1)}, bf16[36,48,96]{2,1,0:T(8,128)(2,1)S(1)}, u32[]{:S(2)}, u32[]{:S(2)}) collective-permute-start(bf16[36,48,96]{2,1,0:T(8,128)(2,1)} %bitcast.27), channel_id=1, source_target_pairs={{0,1},{1,0},{2,3},{3,2},{4,5},{5,4},{6,7},{7,6},{8,9},{9,8},{10,11... | collective-permute-start | bytes 995336 | tf_op jit(solution)/shard_map/ppermute | solution.py:448
  1.2 6.5 %collective-permute-start.2 = (bf16[36,48,96]{2,1,0:T(8,128)(2,1)}, bf16[36,48,96]{2,1,0:T(8,128)(2,1)S(1)}, u32[]{:S(2)}, u32[]{:S(2)}) collective-permute-start(bf16[36,48,96]{2,1,0:T(8,128)(2,1)} %bitcast.30), channel_id=1, source_target_pairs={{0,30},{2,0},{4,2},{6,4},{8,6},{10,8},{12,10},{14,12},{16,14},{18,... | collective-permute-start | bytes 995336 | tf_op jit(solution)/shard_map/ppermute | solution.py:23
  7.7 0.7 %pad_add_fusion = s32[3,96]{1,0:T(4,128)S(1)} fusion(s32[1,6]{1,0:T(1,128)} %link_h.1, s32[1,96]{1,0:T(1,128)} %fresh_h.1, s32[1,96]{1,0:T(1,128)} %bond_h.1), kind=kLoop, calls=%fused_computation | loop fusion | flops 576 | bytes 1944 | tf_op jit(solution)/shard_map/concatenate | solution.py:446
  8.4 0.6 %collective-permute-start = (s32[3,96]{1,0:T(4,128)S(1)}, s32[3,96]{1,0:T(4,128)S(1)}, u32[]{:S(2)}, u32[]{:S(2)}) collective-permute-start(s32[3,96]{1,0:T(4,128)S(1)} %pad_add_fusion), channel_id=1, source_target_pairs={{0,30},{2,0},{4,2},{6,4},{8,6},{10,8},{12,10},{14,12},{16,14},{18,... | collective-permute-start | bytes 3464 | tf_op jit(solution)/shard_map/ppermute | solution.py:23
  9.0 1.0 %reshape.25.ket = bf16[36,72]{1,0:T(8,128)(2,1)S(1)} reshape(bf16[6,6,6,2,6]{4,3,2,1,0:T(2,128)(2,1)} %bitcast.29) | data formatting | bytes 10368 | tf_op jit(solution)/shard_map/reshape | solution.py:451
  10.0 2.1 %prep.1 = (bf16[1920,96]{1,0:T(8,128)(2,1)S(1)}, bf16[432,256]{1,0:T(8,128)(2,1)S(1)}, bf16[80,144]{1,0:T(8,128)(2,1)S(1)}, s32[72,256]{1,0:T(8,128)S(1)}, s32[8...) custom-call(bf16[36,72]{1,0:T(8,128)(2,1)S(1)} %reshape.25.ket, ...), custom_call_target="tpu_custom_call" | custom-call | flops 134217728 | bytes 1048576 | tf_op jit(solution)/shard_map/prep/pallas_call | solution.py:455
  12.1 6.0 %collective-permute-done.charges_s.charges_v = s32[3,96]{1,0:T(4,128)S(1)} collective-permute-done((s32[3,96]{1,0:T(4,128)S(1)}, s32[3,96]{1,0:T(4,128)S(1)}, u32[]{:S(2)}, u32[]{:S(2)}) %collective-permute-start) | collective-permute-done | bytes 1184 | tf_op jit(solution)/shard_map/ppermute | solution.py:23
  18.1 0.0 collective-permute-done.1.other
  18.1 8.5 %front.1 = (bf16[3,3,96,512]{3,2,1,0:T(8,128)(2,1)S(1)}, bf16[432,256]{1,0:T(8,128)(2,1)S(1)}, bf16[80,144]{1,0:T(8,128)(2,1)S(1)}, bf16[18,144,768]{2,1,0:T(8,1...) custom-call(s32[3,96]{1,0:T(4,128)S(1)} %collective-permute-done.charges_s.charges_v, ...), custom_call_target="tpu_custom_call" | custom-call | flops 1073741824 | bytes 1048576 | tf_op jit(solution)/shard_map/front/pallas_call | solution.py:484
  26.6 0.0 collective-permute-done.2.pr_mine
  26.6 0.1 collective-permute-start.3
  26.7 2.8 %middle.1 = (bf16[18,144,768]{2,1,0:T(8,128)(2,1)S(1)}, bf16[6,288,768]{2,1,0:T(8,128)(2,1)S(1)}) custom-call(bf16[1920,96]{1,0:T(8,128)(2,1)S(1)} %get-tuple-element.24.lhs, bf16[3,3,96,512]{3,2,1,0:T(8,128)(2,1)S(1)} %get-tuple-element.32.ms, bf16[432,256]{1,0:T(8,128)(2,1)S(1)} %get-tuple-element.33.k2, bf16[80,144]{1,0:T(8,128)(2,1)S(1)} %get-tuple-element.34.k3, ...), custom_call_target="tpu_custom_call" | custom-call | flops 1073741824 | bytes 1048576 | tf_op jit(solution)/shard_map/middle/pallas_call | solution.py:507
  29.5 0.0 collective-permute-done.3.pr_other
  29.5 11.7 %back.1 = (f32[1728,96]{1,0:T(8,128)S(1)}, f32[32,1,128]{2,1,0:T(1,128)S(1)}) custom-call(s32[3,96]{1,0:T(4,128)S(1)} %collective-permute-done.charges_s.charges_v, s32[3,96]{1,0:T(4,128)S(1)} %collective-permute-done.charges_s.charges_v, bf16[1920,96]{1,0:T(8,128)(2,1)S(1)} %get-tuple-element.24.lhs, bf16[3,3,96,512]{3,2,1,0:T(8,128)(2,1)S(1)} %get-tuple-element.32.ms, ...), custom_call_target="tpu_custom_call" | custom-call | flops 2147483648 | bytes 1048576 | tf_op jit(solution)/shard_map/back/pallas_call | solution.py:518
  41.1 13.4 %all_to_all.5 = f32[32,1,128]{2,1,0:T(1,128)S(1)} all-to-all(f32[32,1,128]{2,1,0:T(1,128)S(1)} %get-tuple-element.42), channel_id=1, replica_groups=mesh['col'=16,'sec'=2] {'col','sec'}, dimensions={0} | all-to-all | bytes 32768 | tf_op jit(solution)/shard_map/all_to_all | solution.py:536
  54.6 0.9 %finish.1 = (bf16[36,48,96]{2,1,0:T(8,128)(2,1)}, f32[1,1]{1,0:T(1,128)}) custom-call(f32[32,128]{1,0:T(8,128)S(1)} %bitcast.25, f32[1728,96]{1,0:T(8,128)S(1)} %get-tuple-element.43.image), custom_call_target="tpu_custom_call" | custom-call | tf_op jit(solution)/shard_map/finish/pallas_call | solution.py:537
Async XLA Ops:
  0.6 17.5 %collective-permute-start.1 = (bf16[36,48,96]{2,1,0:T(8,128)(2,1)}, bf16[36,48,96]{2,1,0:T(8,128)(2,1)S(1)}, u32[]{:S(2)}, u32[]{:S(2)}) collective-permute-start(bf16[36,48,96]{2,1,0:T(8,128)(2,1)} %bitcast.27), channel_id=1, source_target_pairs={{0,1},{1,0},{2,3},{3,2},{4,5},{5,4},{6,7},{7,6},{8,9},{9,8},{10,11... | collective-permute-start | bytes 995336 | tf_op jit(solution)/shard_map/ppermute | solution.py:448
  1.2 25.4 %collective-permute-start.2 = (bf16[36,48,96]{2,1,0:T(8,128)(2,1)}, bf16[36,48,96]{2,1,0:T(8,128)(2,1)S(1)}, u32[]{:S(2)}, u32[]{:S(2)}) collective-permute-start(bf16[36,48,96]{2,1,0:T(8,128)(2,1)} %bitcast.30), channel_id=1, source_target_pairs={{0,30},{2,0},{4,2},{6,4},{8,6},{10,8},{12,10},{14,12},{16,14},{18,... | collective-permute-start | bytes 995336 | tf_op jit(solution)/shard_map/ppermute | solution.py:23
  8.4 9.7 %collective-permute-start = (s32[3,96]{1,0:T(4,128)S(1)}, s32[3,96]{1,0:T(4,128)S(1)}, u32[]{:S(2)}, u32[]{:S(2)}) collective-permute-start(s32[3,96]{1,0:T(4,128)S(1)} %pad_add_fusion), channel_id=1, source_target_pairs={{0,30},{2,0},{4,2},{6,4},{8,6},{10,8},{12,10},{14,12},{16,14},{18,... | collective-permute-start | bytes 3464 | tf_op jit(solution)/shard_map/ppermute | solution.py:23
  26.6 2.9 %collective-permute-start.3 = (bf16[36,48,96]{2,1,0:T(8,128)(2,1)S(1)}, bf16[36,48,96]{2,1,0:T(8,128)(2,1)S(1)}, u32[]{:S(2)}, u32[]{:S(2)}) collective-permute-start(bf16[36,48,96]{2,1,0:T(8,128)(2,1)S(1)} %collective-permute-done.2.pr_mine), channel_id=1, source_target_pairs={{0,1},{1,0},{2,3},{3,2},{4,5},{5,4},{6,7},{7,6},{8,9},{9,8},{10,11... | collective-permute-start | bytes 995336 | tf_op jit(solution)/shard_map/ppermute | solution.py:506
